TPU v7x, 128 devices: a whole 4x4x4 slice. The times are simulated.
128 devices in a mesh: seq: 8 (over y_lo, x), exp: 16 (over y_hi, z, core).
Axes of the slice: x: 4, y: 4 (y_hi: 2, y_lo: 2; y = y_hi * 2 + y_lo), z: 4, core: 2. Of those that a mesh axis runs over, the one named last changes fastest.
Arguments:
- gates: float32 [16384, 2], P(('seq', 'exp')), may hold values from 0.1 to 0.9
- expert_ids: int32 [16384, 2], P(('seq', 'exp')), may hold values from 0 to 15, all different within a row; in each aligned block of 128 rows (0 to 127, 128 to 255, ...) at most 16 rows name the same one
- saved_pre: bfloat16 [16, 2048, 2, 7168], P('exp', None, None, 'seq'), may hold values from -6 to 6
- w_down: bfloat16 [16, 7168, 4096], P('exp', 'seq'), may hold values from -0.0625 to 0.0625
- residual_grad: bfloat16 [16384, 4096], P(('seq', 'exp')), may hold values from -6 to 6
- in_weight: bfloat16 [4096, 4096], P('seq', 'exp'), may hold values from -0.09375 to 0.09375
- ssm_in: bfloat16 [16384, 4096], P('seq', 'exp'), may hold values from -0.59765625 to 0.59765625
- b_proj: bfloat16 [16384, 128], P('seq'), may hold values from -0.546875 to 0.546875
- c_proj: bfloat16 [16384, 128], P('seq'), may hold values from -0.546875 to 0.546875
- step_sizes: float32 [64, 16384], P('exp', 'seq'), may hold values from 0.05 to 4590.52
- a_log: float32 [64], P('exp'), may hold values from -12 to 0
- skip_gain: float32 [64], P('exp'), may hold values from 0.5 to 1.5
- ssm_grad: bfloat16 [16384, 4096], P('seq', 'exp'), may hold values from -6 to 6
Outputs:
- pre_grads: bfloat16 [16, 2048, 2, 7168], P('exp', None, None, 'seq')
- route_grads: float32 [16384, 2], P(('seq', 'exp'))
- b_grads: float32 [16384, 128], P(('seq', 'exp'))
- c_grads: float32 [16384, 128], P(('seq', 'exp'))
- step_grads: float32 [64, 16384], P('exp', 'seq')
Inputs may be any that keep to these rules, and one draw needn't show every extreme that they name: `expert_ids`: in each aligned block of 128 rows every expert is named by exactly 16 entries, and a row names 2 different experts.
All inputs are finite; a program needn't handle non-finite values.
Results may differ from a plain program's by a relative error of at most 0.019.
Values may be sent and summed in bfloat16 or wider, within the bound.
No kernel may reach another device: no remote copies, remote signals or barrier semaphores. Data moves between devices by JAX's collectives and lax.ppermute only.
A program may use at most 192 MiB of HBM per device.

v0:
```python
import functools
import jax
import jax.numpy as jnp
from jax import lax
from jax.experimental import pallas as pl
from jax.experimental.pallas import tpu as pltpu
from jax.sharding import Mesh
from jax.sharding import PartitionSpec as P

F32 = jnp.float32
BF = jnp.bfloat16
HEADS, HDIM, NST, L = 4, 64, 128, 128
HP = HEADS * HDIM
NT = (((1,), (1,)), ((), ()))
TN = (((0,), (0,)), ((), ()))


def dot(a, b, dims=(((1,), (0,)), ((), ())), precision=None):
    return lax.dot_general(a, b, dims, precision=precision, preferred_element_type=F32)


def cost(us):
    return pl.CostEstimate(flops=int(us * 5e8), bytes_accessed=1 << 20, transcendentals=0)


def over_heads(cols):
    low = lax.broadcasted_iota(jnp.int32, (cols.shape[0], 128), 1) < HDIM
    return jnp.concatenate(
        [jnp.where(low, cols[:, h : h + 1], cols[:, h + 1 : h + 2]) for h in (0, 2)], axis=1
    )


def head_rows(rows):
    return jnp.concatenate(
        [jnp.broadcast_to(rows[h : h + 1, :], (HDIM, NST)) for h in range(HEADS)], axis=0
    )


def states_kernel(
    x_ref, g_ref, b_ref, c_ref, step_ref, alog_ref,
    cumr_ref, cumc_ref, sl_ref, gl_ref, dpre_ref, dpost_ref, pack_ref, q_ref,
):
    spans = sl_ref.shape[0]
    q_ref[...] = jnp.zeros_like(q_ref)
    q = step_ref[...] * jnp.exp(alog_ref[...])
    for c in range(spans):
        q_ref[8 * c : 8 * c + HEADS, :] = q[:, L * c : L * (c + 1)]
    row = lax.broadcasted_iota(jnp.int32, (L, L), 0)
    col = lax.broadcasted_iota(jnp.int32, (L, L), 1)
    upper = (row <= col).astype(F32)
    cum = dot(q_ref[...], upper, precision=lax.Precision.HIGHEST)
    cumr_ref[...] = cum.reshape(spans, 8, L)
    turned = cum.T
    for c in range(spans):
        cumc_ref[c] = turned[:, 8 * c : 8 * c + 8]

    def forward(c, carry):
        state, run = carry
        sl_ref[c] = state.astype(BF)
        dpre_ref[c] = jnp.exp(-run)
        at = pl.ds(pl.multiple_of(c * L, L), L)
        cols = cumc_ref[c]
        last = jnp.broadcast_to(cumr_ref[c][:, L - 1 : L], (8, NST))
        tail = jnp.exp(jnp.minimum(cols - cols[L - 1 : L, :], 0.0))
        decayed = (x_ref[at, :].astype(F32) * over_heads(tail)).astype(BF)
        fresh = dot(decayed, b_ref[at, :], TN)
        return (head_rows(jnp.exp(-last)) * state + fresh, run + last)

    zero = (jnp.zeros((HP, NST), F32), jnp.zeros((8, NST), F32))
    state, run = lax.fori_loop(0, spans, forward, zero)
    pack_ref[0:HP, :] = state.astype(BF)
    total = jnp.exp(-run)
    high = total.astype(BF).astype(F32)
    pack_ref[2 * HP : 2 * HP + 16, :] = jnp.concatenate([high, total - high], axis=0).astype(BF)

    def backward(i, carry):
        state, run = carry
        c = spans - 1 - i
        gl_ref[c] = state.astype(BF)
        dpost_ref[c] = jnp.exp(-run)
        at = pl.ds(pl.multiple_of(c * L, L), L)
        last = jnp.broadcast_to(cumr_ref[c][:, L - 1 : L], (8, NST))
        decayed = (g_ref[at, :].astype(F32) * over_heads(jnp.exp(-cumc_ref[c]))).astype(BF)
        fresh = dot(decayed, c_ref[at, :], TN)
        return (head_rows(jnp.exp(-last)) * state + fresh, run + last)

    state, run = lax.fori_loop(0, spans, backward, zero)
    pack_ref[HP : 2 * HP, :] = state.astype(BF)


def local_states(x, g, b, c, step, alog):
    spans = x.shape[0] // L
    out = (
        jax.ShapeDtypeStruct((spans, 8, L), F32),
        jax.ShapeDtypeStruct((spans, L, 8), F32),
        jax.ShapeDtypeStruct((spans, HP, NST), BF),
        jax.ShapeDtypeStruct((spans, HP, NST), BF),
        jax.ShapeDtypeStruct((spans, 8, NST), F32),
        jax.ShapeDtypeStruct((spans, 8, NST), F32),
        jax.ShapeDtypeStruct((2 * HP + 16, NST), BF),
    )
    return pl.pallas_call(
        states_kernel,
        out_shape=out,
        scratch_shapes=[pltpu.VMEM((8 * spans, L), F32)],
        cost_estimate=cost(16),
        name="states",
    )(x, g, b, c, step, alog)


def grads_kernel(
    me_ref, x_ref, g_ref, b_ref, c_ref, cumr_ref, cumc_ref, sl_ref, gl_ref, dpre_ref, dpost_ref,
    packs_ref, alog_ref, skip_ref,
    dx_ref, bc_ref, dq_ref, sin_ref, gex_ref,
):
    count = packs_ref.shape[0]

    @pl.when(pl.program_id(0) == 0)
    def _():
        me = me_ref[0]

        def dec(s):
            both = packs_ref[s, HP : HP + 16, :].astype(F32)
            return head_rows(both[0:8] + both[8:16])

        sin_ref[...] = jnp.zeros_like(sin_ref)
        gex_ref[...] = jnp.zeros_like(gex_ref)
        for s in range(count):
            @pl.when(s < me)
            def _():
                sin_ref[...] = dec(s) * sin_ref[...] + packs_ref[s, 0:HP, :].astype(F32)
        for s in reversed(range(count)):
            @pl.when(s > me)
            def _():
                gex_ref[...] = dec(s) * gex_ref[...] + packs_ref[s, 0:HP, :].astype(F32)

    x = x_ref[...]
    g = g_ref[...]
    b = b_ref[...]
    c = c_ref[...]
    xf = x.astype(F32)
    gf = g.astype(F32)
    rows = cumr_ref[0]
    cols = cumc_ref[0]
    state = sl_ref[0].astype(F32) + head_rows(dpre_ref[0]) * sin_ref[...]
    after = gl_ref[0].astype(F32) + head_rows(dpost_ref[0]) * gex_ref[...]
    state_b = state.astype(BF)
    after_b = after.astype(BF)
    into = over_heads(jnp.exp(-cols))
    tail = over_heads(jnp.exp(jnp.minimum(cols - cols[L - 1 : L, :], 0.0)))
    g_in = (gf * into).astype(BF)
    x_tail = (xf * tail).astype(BF)
    dc = dot(g_in, state_b)
    db = dot(x_tail, after_b)
    from_after = dot(b, after_b, NT) * tail
    carried = dot(c, state_b, NT) * into
    scores = dot(c, b, NT)
    row = lax.broadcasted_iota(jnp.int32, (L, L), 0)
    col = lax.broadcasted_iota(jnp.int32, (L, L), 1)
    lower = row >= col
    before = (row < col).astype(BF)
    lower_b = lower.astype(BF)
    picks = (
        lax.broadcasted_iota(jnp.int32, (8, HP), 1) // HDIM
        == lax.broadcasted_iota(jnp.int32, (8, HP), 0)
    ).astype(BF)
    late = dot(picks, (gf * carried).astype(BF), NT)
    early = dot(picks, (xf * from_after).astype(BF), NT)
    across = jnp.sum(dot(picks, (state * after).astype(BF)), axis=1, keepdims=True)
    steps = (
        dot(late.astype(BF), lower_b)
        + dot(early.astype(BF), before)
        + across * jnp.exp(-rows[:, L - 1 : L])
    )
    mixed = jnp.zeros((L, L), F32)
    inner = []
    pieces = []
    for h in range(HEADS):
        at = slice(HDIM * h, HDIM * (h + 1))
        g_h = g[:, at]
        cross = dot(g_h, x[:, at], NT)
        decay = jnp.where(
            lower, jnp.exp(jnp.minimum(rows[h : h + 1, :] - cols[:, h : h + 1], 0.0)), 0.0
        )
        kept = decay * cross
        mixed = mixed + kept
        pieces.append(dot((decay * scores).astype(BF), g_h, TN))
        passed = dot((kept * scores).astype(BF), before)
        inner.append(jnp.sum(jnp.where(lower, passed, 0.0), axis=0, keepdims=True))
    steps = steps[0:HEADS] + jnp.concatenate(inner, axis=0)
    dq_ref[...] = -steps * jnp.exp(alog_ref[...])
    dx = jnp.concatenate(pieces, axis=1) + from_after + gf * skip_ref[...]
    dx_b = dx.astype(dx_ref.dtype)
    for q in range(dx_ref.shape[0]):
        dx_ref[q, 0, 0] = dx_b
    mixed_b = mixed.astype(BF)
    bc_ref[:, 0:NST] = (db + dot(mixed_b, c, TN)).astype(bc_ref.dtype)
    bc_ref[:, NST:] = (dc + dot(mixed_b, b)).astype(bc_ref.dtype)


def span_grads(me, x, g, b, c, parts, packs, alog, skip, half):
    cumr, cumc, sl, gl, dpre, dpost = parts
    spans = sl.shape[0] // 2
    base = half * spans
    once = lambda shape: pl.BlockSpec(shape, lambda i: (0,) * len(shape))
    lead = lambda shape: pl.BlockSpec((1, *shape), lambda i: (base + i, 0, 0))
    rows = lambda width: pl.BlockSpec((L, width), lambda i: (base + i, 0))
    return pl.pallas_call(
        grads_kernel,
        grid=(spans,),
        in_specs=[
            pl.BlockSpec(memory_space=pltpu.SMEM),
            rows(HP), rows(HP), rows(NST), rows(NST),
            lead((8, L)), lead((L, 8)), lead((HP, NST)), lead((HP, NST)),
            lead((8, NST)), lead((8, NST)),
            once(packs.shape), once(alog.shape), once(skip.shape),
        ],
        out_specs=[
            pl.BlockSpec((4, 1, 1, L, HP), lambda i: (0, i % 4, i // 4, 0, 0)),
            pl.BlockSpec((L, 2 * NST), lambda i: (i, 0)),
            pl.BlockSpec((HEADS, L), lambda i: (0, i)),
        ],
        out_shape=(
            jax.ShapeDtypeStruct((4, 4, spans // 4, L, HP), BF),
            jax.ShapeDtypeStruct((spans * L, 2 * NST), BF),
            jax.ShapeDtypeStruct((HEADS, spans * L), F32),
        ),
        scratch_shapes=[pltpu.VMEM((HP, NST), F32), pltpu.VMEM((HP, NST), F32)],
        cost_estimate=cost(10),
        name="span_grads",
    )(me, x, g, b, c, cumr, cumc, sl, gl, dpre, dpost, packs, alog, skip)


def routing_kernel(ids_ref, gates_ref, tgt_ref, out_ref):
    experts, slots = out_ref.shape
    tokens = ids_ref.shape[1]
    expert = lax.broadcasted_iota(jnp.int32, (experts, tokens), 0)
    slot = lax.broadcasted_iota(jnp.int32, (slots, tokens), 0)
    named = [(expert == ids_ref[k : k + 1, :]).astype(F32) for k in range(2)]
    earlier = (
        lax.broadcasted_iota(jnp.int32, (tokens, tokens), 0)
        < lax.broadcasted_iota(jnp.int32, (tokens, tokens), 1)
    ).astype(BF)
    counts = dot((named[0] + named[1]).astype(BF), earlier)
    tgt_ref[...] = jnp.zeros_like(tgt_ref)
    total = jnp.zeros((experts, slots), F32)
    for k in range(2):
        position = jnp.sum(named[k] * counts, axis=0, keepdims=True).astype(jnp.int32)
        tgt_ref[k : k + 1, :] = ids_ref[k : k + 1, :] * slots + position
        placed = (slot == position).astype(BF)
        total = total + dot((named[k] * gates_ref[k : k + 1, :]).astype(BF), placed, NT)
    out_ref[...] = total.astype(out_ref.dtype)


def routing(ids, gates):
    return pl.pallas_call(
        routing_kernel,
        out_shape=(
            jax.ShapeDtypeStruct((8, ids.shape[1]), jnp.int32),
            jax.ShapeDtypeStruct((16, 16), BF),
        ),
        cost_estimate=cost(2),
        name="routing",
    )(ids, gates)


def first_kernel(res_ref, tgt_ref, w_ref, out_ref):
    named = tgt_ref[...].astype(F32)
    named = jnp.concatenate([named, jnp.zeros_like(named)], axis=0).astype(BF)
    for q in range(4):
        for s in range(8):
            lanes = slice(128 * s, 128 * (s + 1))
            out_ref[q, 0:128, lanes] = res_ref[:, 512 * s + 128 * q : 512 * s + 128 * (q + 1)]
            out_ref[q, 128:144, lanes] = named
        for j in range(4):
            rows = slice(128 * q + 32 * j, 128 * q + 32 * (j + 1))
            out_ref[q, 144:176, 256 * j : 256 * (j + 1)] = w_ref[rows, :]


def first_exchange(residual, targets, weight):
    return pl.pallas_call(
        first_kernel,
        out_shape=jax.ShapeDtypeStruct((4, 176, 1024), BF),
        cost_estimate=cost(3),
        name="first_exchange",
    )(residual, targets, weight)


def rows_kernel(x_ref, w_ref, res_ref, out_ref, acc_ref):
    def step(e, carry):
        blocks = [w_ref[s, e % 4, e // 4] for s in range(2)]
        right = jnp.concatenate(
            [block[:, 256 * j : 256 * (j + 1)] for block in blocks for j in range(4)], axis=0
        )
        acc_ref[...] += dot(x_ref[e], right, NT)
        return carry

    acc_ref[...] = jnp.zeros_like(acc_ref)
    lax.fori_loop(0, 16, step, 0, unroll=16)
    slot = lax.broadcasted_iota(jnp.int32, (256, 128), 0).astype(F32)
    for k in range(2):
        total = acc_ref[128 * k : 128 * (k + 1), :]
        rows = (res_ref[k, 0:128, :].astype(F32) + total).astype(BF)
        named = res_ref[k, 128:144, 0:128].astype(F32)
        picks = (slot == named[0:1, :]) | (slot == named[1:2, :])
        out_ref[:, k] = dot(picks.astype(BF), rows).astype(BF).reshape(16, 16, 256)


def expert_rows(x, weight, residual, half):
    return pl.pallas_call(
        rows_kernel,
        grid=(4,),
        in_specs=[
            pl.BlockSpec((16, 256, 256), lambda s: (0, 0, 0)),
            pl.BlockSpec((2, 4, 4, 32, 1024), lambda s: (s, 0, 0, 0, 0)),
            pl.BlockSpec((2, 144, 256), lambda s: (half, 0, s)),
        ],
        out_specs=pl.BlockSpec((16, 2, 16, 256), lambda s: (0, 0, 0, s)),
        out_shape=jax.ShapeDtypeStruct((16, 2, 16, 1024), BF),
        scratch_shapes=[pltpu.VMEM((256, 256), F32)],
        compiler_params=pltpu.CompilerParams(vmem_limit_bytes=48 << 20),
        cost_estimate=cost(6),
        name="expert_rows",
    )(x, weight, residual)


def turned_kernel(w_ref, out_ref):
    for q in range(4):
        for s in range(8):
            out_ref[:, 1024 * q + 128 * s : 1024 * q + 128 * (s + 1)] = w_ref[
                :, 512 * s + 128 * q : 512 * s + 128 * (q + 1)
            ]


def turned(w):
    rows = 128
    spec = pl.BlockSpec((rows, w.shape[1]), lambda i: (i, 0))
    return pl.pallas_call(
        turned_kernel,
        grid=(w.shape[0] // rows,),
        in_specs=[spec],
        out_specs=spec,
        out_shape=jax.ShapeDtypeStruct(w.shape, w.dtype),
        cost_estimate=cost(6),
        name="turned",
    )(w)


def expert_kernel(half, at_ref, own, left, right, low, high, w_hbm, saved, gates, *rest):
    out, route_ref, xbuf, wbuf, sbuf, gbuf, obuf, up_ref, psum_ref, mixed_ref, grad_ref, sems = rest[
        -12:
    ]
    x_at, y_at = at_ref[0], at_ref[1]
    saved_copy = pltpu.make_async_copy(saved.at[y_at, :, half], sbuf.reshape(4, 128, 2, 896), sems.at[4])
    gates_copy = pltpu.make_async_copy(gates.at[y_at, :, half], gbuf.reshape(4, 128, 1), sems.at[5])
    weights = [
        pltpu.make_async_copy(
            w_hbm.at[256 * i : min(256 * (i + 1), 896), :],
            wbuf.at[256 * i : min(256 * (i + 1), 896), :],
            sems.at[i],
        )
        for i in range(4)
    ]
    copies = []
    for piece, step, first in ((own, 0, 0), (left, 3, 0), (right, 1, 0), (low, 2, 0), (high, 2, 2)):
        source = lax.rem(x_at + step, 4)
        for q in range(piece.shape[0]):
            for k in range(2):
                copies.append(
                    pltpu.make_async_copy(
                        piece.at[q, :, k],
                        xbuf.at[first + q, source, k],
                        sems.at[6 + len(copies)],
                    )
                )
    weights[0].start()
    for copy in copies:
        copy.start()
    for copy in weights[1:]:
        copy.start()
    gates_copy.start()
    saved_copy.start()
    for copy in copies:
        copy.wait()

    def tile(at, width):
        here = pl.ds(at, width)
        up_ref[:, here] = jnp.zeros((512, width), F32)

        def step(q, carry):
            piece = xbuf[q].reshape(512, 1024)
            lanes = pl.ds(pl.multiple_of(q * 1024, 1024), 1024)
            up_ref[:, here] += dot(piece, wbuf[here, lanes], NT)
            return carry

        lax.fori_loop(0, 4, step, 0)

    def later(i, carry):
        tile(pl.multiple_of(i * 256, 256), 256)
        return carry

    weights[0].wait()
    tile(0, 256)
    for copy in (weights[1], weights[2], weights[3]):
        copy.wait()
    lax.fori_loop(1, 3, later, 0)
    tile(768, 128)
    gates_copy.wait()
    saved_copy.wait()
    count = 32

    def group(j, carry):
        rows = pl.ds(pl.multiple_of(j * count, count), count)
        gate = gbuf[rows, :]
        routed = jnp.zeros((count, 128), F32)
        for n in range(7):
            lanes = slice(128 * n, 128 * (n + 1))
            mixed_ref[...] = sbuf[rows, :, lanes].reshape(2 * count, 128).astype(F32)
            gate_pre = mixed_ref[pl.ds(0, count, stride=2), :]
            up_pre = mixed_ref[pl.ds(1, count, stride=2), :]
            upstream = up_ref[rows, lanes]
            sigmoid = 1.0 / (1.0 + jnp.exp(-gate_pre))
            active = gate_pre * sigmoid
            weighted = gate * upstream
            routed = routed + active * up_pre * upstream
            grad_ref[pl.ds(0, count, stride=2), :] = (
                weighted * up_pre * sigmoid * (1.0 + gate_pre * (1.0 - sigmoid))
            )
            grad_ref[pl.ds(1, count, stride=2), :] = weighted * active
            obuf[rows, :, lanes] = grad_ref[...].astype(BF).reshape(count, 2, 128)
        psum_ref[rows, :] = routed
        return carry

    lax.fori_loop(0, 512 // count, group, 0)
    out_copy = pltpu.make_async_copy(obuf.reshape(4, 128, 2, 896), out.at[y_at, :, half], sems.at[4])
    out_copy.start()
    ones = jnp.ones((8, 128), F32)
    route_ref[...] = dot(ones, psum_ref[...], NT, precision=lax.Precision.HIGHEST)
    out_copy.wait()


def expert_grads(half, at, pieces, weight, saved, gates, before):
    own, left, right, low, high = [p.reshape(-1, 4, 2, 16, 1024) for p in pieces]
    hbm = pl.BlockSpec(memory_space=pl.ANY)
    args = [at, own, left, right, low, high, weight, saved, gates]
    if before is not None:
        args.append(before)
    return pl.pallas_call(
        functools.partial(expert_kernel, half),
        in_specs=[pl.BlockSpec(memory_space=pltpu.SMEM)] + [hbm] * (len(args) - 1),
        out_specs=[hbm, pl.BlockSpec(memory_space=pltpu.VMEM)],
        out_shape=(
            jax.ShapeDtypeStruct(saved.shape, BF),
            jax.ShapeDtypeStruct((8, 512), F32),
        ),
        scratch_shapes=[
            pltpu.VMEM((4, 4, 2, 4, 16, 1024), BF),
            pltpu.VMEM((896, 4096), BF),
            pltpu.VMEM((512, 2, 896), BF),
            pltpu.VMEM((512, 1), F32),
            pltpu.VMEM((512, 2, 896), BF),
            pltpu.VMEM((512, 896), F32),
            pltpu.VMEM((512, 128), F32),
            pltpu.VMEM((64, 128), F32),
            pltpu.VMEM((64, 128), F32),
            pltpu.SemaphoreType.DMA((40,)),
        ],
        input_output_aliases={} if before is None else {9: 0},
        compiler_params=pltpu.CompilerParams(vmem_limit_bytes=56 << 20),
        cost_estimate=cost(12),
        name="expert_grads",
    )(*args)


SEQ = ("yl", "x")
QUAD = ("yh", "zh")
MEMB = ("zl", "core")
EXP = QUAD + MEMB
BOTH = SEQ + EXP


def a2a(array, axis):
    return lax.all_to_all(array, axis, split_axis=0, concat_axis=0, tiled=True)


def shifted(array, by):
    return lax.ppermute(array, "x", [(i, (i + by) % 4) for i in range(4)])


def other_row(array):
    return lax.ppermute(array, "yl", [(0, 1), (1, 0)])


def along_x(own):
    return joined_x((own, shifted(own, 1), shifted(own, -1)))


def joined_x(pieces):
    own, left, right = pieces
    low = shifted(left[:8], 1)
    high = shifted(right[8:], -1)
    return (own, left, right, low, high)


def per_device(
    gates, expert_ids, saved_pre, w_down, residual_grad, in_weight,
    ssm_in, b_proj, c_proj, step_sizes, a_log, skip_gain, ssm_grad,
):
    targets, slot_gates = routing(expert_ids.T, gates.T)
    first = first_exchange(residual_grad, targets, in_weight)
    first = a2a(first, QUAD)
    weight = lax.all_gather(first[:, 144:176].reshape(128, 1024), SEQ + MEMB, axis=0, tiled=True)
    weight = weight.reshape(8, 4, 4, 32, 1024)

    alog = a_log.reshape(4, 1)
    skip = jnp.repeat(skip_gain, HDIM).reshape(1, HP)
    *parts, pack = local_states(ssm_in, ssm_grad, b_proj, c_proj, step_sizes, alog)
    first, pack = lax.optimization_barrier((first, pack))
    here = lax.axis_index(SEQ)
    later = lax.broadcasted_iota(jnp.int32, (8, HP, NST), 0) > here
    states = jnp.where(later, pack[:HP], pack[HP : 2 * HP])
    rest = jnp.concatenate([pack[2 * HP :], jnp.pad(slot_gates, ((0, 0), (0, 112)))], axis=0)
    packs = jnp.concatenate([states, jnp.broadcast_to(rest, (8, *rest.shape))], axis=1)
    packs = a2a(packs, SEQ)
    gate_rows = packs[:, HP + 16 :, 0:16].transpose(1, 0, 2)
    gate_rows = a2a(gate_rows.reshape(16, 128), EXP)
    down = turned(w_down[0])

    args = (here.reshape(1), ssm_in, ssm_grad, b_proj, c_proj, parts, packs, alog, skip)
    arrived, grads = {}, {}
    for half in (1, 0):
        x_part, bc_part, step_part = span_grads(*args, half)
        grads[half] = (bc_part, step_part)
        if half == 1:
            x_part, gate_rows = lax.optimization_barrier((x_part, gate_rows))
        moved = a2a(x_part.reshape(16, 256, 256), EXP)
        rows = expert_rows(moved, weight, first, half)
        arrived[half] = a2a(rows.reshape(16, 32, 1024), EXP)

    gate_rows = gate_rows.reshape(16, 8, 16).transpose(1, 0, 2)
    gate_rows = gate_rows.astype(F32).reshape(2, 4, 2, 128, 1)
    near = (arrived[1], shifted(arrived[1], 1), shifted(arrived[1], -1))
    across = other_row(arrived[1])
    mine = joined_x(near)
    theirs = joined_x((across, other_row(near[1]), other_row(near[2])))
    partner = other_row(arrived[0])
    sets = [(1, 0, mine), (0, 0, along_x(arrived[0])), (1, 1, theirs), (0, 1, along_x(partner))]

    x_at, y_at = lax.axis_index("x"), lax.axis_index("yl")
    saved = saved_pre.reshape(2, 4, 2, 128, 2, 896)
    out, routes = None, {}
    for half, flip, pieces in sets:
        at = jnp.stack([x_at, y_at ^ flip]).astype(jnp.int32)
        out, route = expert_grads(half, at, pieces, down, saved, gate_rows, out)
        routes[half, flip] = route[0].reshape(4, 128)
    first, second = [
        jnp.stack([routes[0, flip], routes[1, flip]], axis=1).reshape(4, 256) for flip in (0, 1)
    ]
    low, high = [jnp.where(y_at == 0, a, b) for a, b in ((first, second), (second, first))]
    partial = jnp.concatenate([low, high], axis=0)
    summed = jnp.sum(a2a(partial, SEQ), axis=0)
    totals = a2a(summed.reshape(16, 16), EXP).reshape(256, 1)
    slot = lax.broadcasted_iota(jnp.int32, (256, 128), 0)
    route_grads = jnp.stack(
        [jnp.sum(jnp.where(slot == targets[k], totals, 0.0), axis=0) for k in range(2)], axis=1
    )

    both = jnp.concatenate([grads[0][0], grads[1][0]], axis=0).reshape(16, 128, 2 * NST)
    both = jnp.sum(a2a(both, EXP).astype(F32), axis=0)
    step_grads = jnp.concatenate([grads[0][1], grads[1][1]], axis=1)
    pre_grads = out.reshape(1, 2048, 2, 896)
    return (pre_grads, route_grads, both[:, :NST], both[:, NST:], step_grads)


def solution(mesh):
    split = Mesh(mesh.devices.reshape(2, 4, 2, 2, 2, 2), BOTH)
    in_specs = (
        P(BOTH, None), P(BOTH, None), P(EXP, None, None, SEQ), P(EXP, SEQ, None), P(BOTH, None),
        P(SEQ, EXP), P(SEQ, EXP), P(SEQ, None), P(SEQ, None), P(EXP, SEQ), P(EXP), P(EXP),
        P(SEQ, EXP),
    )
    out_specs = (P(EXP, None, None, SEQ), P(BOTH, None), P(BOTH, None), P(BOTH, None), P(EXP, SEQ))

    return jax.shard_map(per_device, mesh=split, in_specs=in_specs, out_specs=out_specs, check_vma=False)
```

profile of v0, /device:TPU:1, one launch (start us, length us, event | category | flops | bytes accessed | tf_op | source)
XLA Modules:
  0.0 407.4 jit_solution(18269034177380528270)
XLA Ops:
  7.2 1.6 routing.1
  8.8 2.6 first_exchange.1
  11.4 28.6 %all_to_all.66.res_ref = bf16[4,176,1024]{2,1,0:T(8,128)(2,1)S(1)} all-to-all(bf16[4,176,1024]{2,1,0:T(8,128)(2,1)} %first_exchange.1), channel_id=1, replica_groups=mesh['yl'=2,'x'=4,'yh'=2,'zh'=2,'zl'=2,'core'=2] {'yh','zh'}, dimensions={0} | all-to-all | bytes 2883584 | tf_op jit(solution)/shard_map/all_to_all | solution.py:483
  41.4 15.6 %states.1 = (f32[16,8,128]{2,1,0:T(8,128)}, f32[16,128,8]{2,1,0:T(8,128)}, bf16[16,256,128]{2,1,0:T(8,128)(2,1)}, bf16[16,256,128]{2,1,0:T(8,128)(2,1)}, f32[16,...) custom-call(bf16[2048,256]{1,0:T(8,128)(2,1)} %x_ref.5, bf16[2048,256]{1,0:T(8,128)(2,1)} %g_ref.5, ...), custom_call_target="tpu_custom_call" | custom-call | flops 8000000000 | bytes 1048576 | tf_op jit(solution)/shard_map/states/pallas_call | solution.py:102
  59.6 4.1 %all-to-all-start.1 = ((bf16[8,288,128]{2,1,0:T(8,128)(2,1)}), bf16[8,288,128]{2,1,0:T(8,128)(2,1)S(1)}, u32[]{:S(2)}, u32[]{:S(2)}) async-start(bf16[8,288,128]{2,1,0:T(8,128)(2,1)} %pad_maximum_fusion.1), calls=%async_computation.1 | async-start | bytes 1179648 | tf_op jit(solution)/shard_map/all_to_all | solution.py:483
  64.5 11.8 %all-to-all-done.1.packs_ref = bf16[8,288,128]{2,1,0:T(8,128)(2,1)S(1)} async-done(((bf16[8,288,128]{2,1,0:T(8,128)(2,1)}), bf16[8,288,128]{2,1,0:T(8,128)(2,1)S(1)}, u32[]{:S(2)}, u32[]{:S(2)}) %all-to-all-start.1) | async-done | bytes 589856 | tf_op jit(solution)/shard_map/all_to_all | solution.py:483
  77.1 6.3 %all-to-all-start.4 = ((bf16[16,1,128]{2,1,0:T(2,128)(2,1)}), bf16[16,1,128]{2,1,0:T(2,128)(2,1)S(1)}, u32[]{:S(2)}, u32[]{:S(2)}) async-start(bf16[16,1,128]{2,1,0:T(2,128)(2,1)} %all_to_all.55), calls=%async_computation.4 | async-start | bytes 16384 | tf_op jit(solution)/shard_map/all_to_all | solution.py:483
  83.4 10.4 %span_grads.3 = (bf16[4,4,2,128,256]{4,3,2,1,0:T(8,128)(2,1)}, bf16[1024,256]{1,0:T(8,128)(2,1)}, f32[4,1024]{1,0:T(4,128)}) custom-call(s32[1]{0:T(128)} %bitcast.2.me_ref, bf16[2048,256]{1,0:T(8,128)(2,1)} %x_ref.5, bf16[2048,256]{1,0:T(8,128)(2,1)} %g_ref.5, bf16[2048,128]{1,0:T(8,128)(2,1)} %b_ref.5, bf16[2048,128]{1,0:T(8,128)(2,1)} %c_ref.5, ...), custom_call_target="tpu_custom_call" | custom-call | flops 5000000000 | bytes 1048576 | tf_op jit(solution)/shard_map/span_grads/pallas_call | solution.py:208
  93.8 7.3 %all-to-all-start.5 = ((bf16[16,256,256]{2,1,0:T(8,128)(2,1)}), bf16[16,256,256]{2,1,0:T(8,128)(2,1)S(1)}, u32[]{:S(2)}, u32[]{:S(2)}) async-start(bf16[16,256,256]{2,1,0:T(8,128)(2,1)} %bitcast.71), calls=%async_computation.5 | async-start | bytes 4194304 | tf_op jit(solution)/shard_map/all_to_all | solution.py:483
  101.1 10.3 %span_grads.2 = (bf16[4,4,2,128,256]{4,3,2,1,0:T(8,128)(2,1)}, bf16[1024,256]{1,0:T(8,128)(2,1)}, f32[4,1024]{1,0:T(4,128)}) custom-call(s32[1]{0:T(128)} %bitcast.2.me_ref, bf16[2048,256]{1,0:T(8,128)(2,1)} %x_ref.5, bf16[2048,256]{1,0:T(8,128)(2,1)} %g_ref.5, bf16[2048,128]{1,0:T(8,128)(2,1)} %b_ref.5, bf16[2048,128]{1,0:T(8,128)(2,1)} %c_ref.5, ...), custom_call_target="tpu_custom_call" | custom-call | flops 5000000000 | bytes 1048576 | tf_op jit(solution)/shard_map/span_grads/pallas_call | solution.py:208
  111.4 18.1 %all-to-all-done.5.x_ref = bf16[16,256,256]{2,1,0:T(8,128)(2,1)S(1)} async-done(((bf16[16,256,256]{2,1,0:T(8,128)(2,1)}), bf16[16,256,256]{2,1,0:T(8,128)(2,1)S(1)}, u32[]{:S(2)}, u32[]{:S(2)}) %all-to-all-start.5) | async-done | bytes 2097184 | tf_op jit(solution)/shard_map/all_to_all | solution.py:483
  129.5 7.6 %all-to-all-start.2 = ((bf16[16,256,256]{2,1,0:T(8,128)(2,1)}), bf16[16,256,256]{2,1,0:T(8,128)(2,1)}, u32[]{:S(2)}, u32[]{:S(2)}) async-start(bf16[16,256,256]{2,1,0:T(8,128)(2,1)} %bitcast.72), calls=%async_computation.2 | async-start | bytes 4194304 | tf_op jit(solution)/shard_map/all_to_all | solution.py:483
  137.1 6.5 %expert_rows.3 = bf16[16,2,16,1024]{3,2,1,0:T(8,128)(2,1)S(1)} custom-call(bf16[16,256,256]{2,1,0:T(8,128)(2,1)S(1)} %all-to-all-done.5.x_ref, bf16[8,4,4,32,1024]{4,3,2,1,0:T(8,128)(2,1)} %bitcast.63, bf16[4,176,1024]{2,1,0:T(8,128)(2,1)S(1)} %all_to_all.66.res_ref), custom_call_target="tpu_custom_call" | custom-call | flops 3000000000 | bytes 1048576 | tf_op jit(solution)/shard_map/expert_rows/pallas_call | solution.py:310
  144.6 21.0 %all-to-all-done.2.x_ref = bf16[16,256,256]{2,1,0:T(8,128)(2,1)} async-done(((bf16[16,256,256]{2,1,0:T(8,128)(2,1)}), bf16[16,256,256]{2,1,0:T(8,128)(2,1)}, u32[]{:S(2)}, u32[]{:S(2)}) %all-to-all-start.2) | async-done | bytes 2097184 | tf_op jit(solution)/shard_map/all_to_all | solution.py:483
  165.5 6.9 %all-to-all-start.6 = ((bf16[16,32,1024]{2,1,0:T(8,128)(2,1)}), bf16[16,32,1024]{2,1,0:T(8,128)(2,1)S(1)}, u32[]{:S(2)}, u32[]{:S(2)}) async-start(bf16[16,32,1024]{2,1,0:T(8,128)(2,1)} %bitcast.57), calls=%async_computation.6 | async-start | bytes 2097152 | tf_op jit(solution)/shard_map/all_to_all | solution.py:483
  172.5 7.9 %expert_rows.2 = bf16[16,2,16,1024]{3,2,1,0:T(8,128)(2,1)} custom-call(bf16[16,256,256]{2,1,0:T(8,128)(2,1)} %all-to-all-done.2.x_ref, bf16[8,4,4,32,1024]{4,3,2,1,0:T(8,128)(2,1)} %bitcast.64, bf16[4,176,1024]{2,1,0:T(8,128)(2,1)S(1)} %all_to_all.66.res_ref), custom_call_target="tpu_custom_call" | custom-call | flops 3000000000 | bytes 1048576 | tf_op jit(solution)/shard_map/expert_rows/pallas_call | solution.py:310
  180.4 9.2 %all-to-all-done.6 = bf16[16,32,1024]{2,1,0:T(8,128)(2,1)S(1)} async-done(((bf16[16,32,1024]{2,1,0:T(8,128)(2,1)}), bf16[16,32,1024]{2,1,0:T(8,128)(2,1)S(1)}, u32[]{:S(2)}, u32[]{:S(2)}) %all-to-all-start.6) | async-done | bytes 1048608 | tf_op jit(solution)/shard_map/all_to_all | solution.py:483
  190.5 4.5 %all-to-all-start.3 = ((bf16[16,32,1024]{2,1,0:T(8,128)(2,1)}), bf16[16,32,1024]{2,1,0:T(8,128)(2,1)S(1)}, u32[]{:S(2)}, u32[]{:S(2)}) async-start(bf16[16,32,1024]{2,1,0:T(8,128)(2,1)} %bitcast.9), calls=%async_computation.3 | async-start | bytes 2097152 | tf_op jit(solution)/shard_map/all_to_all | solution.py:483
  195.0 3.8 collective-permute-start.6
  198.8 2.2 collective-permute-start.8
  201.0 11.2 %all-to-all-done.3 = bf16[16,32,1024]{2,1,0:T(8,128)(2,1)S(1)} async-done(((bf16[16,32,1024]{2,1,0:T(8,128)(2,1)}), bf16[16,32,1024]{2,1,0:T(8,128)(2,1)S(1)}, u32[]{:S(2)}, u32[]{:S(2)}) %all-to-all-start.3) | async-done | bytes 1048608 | tf_op jit(solution)/shard_map/all_to_all | solution.py:483
  212.2 3.8 collective-permute-start.12
  216.0 2.1 collective-permute-start.13
  218.8 5.7 %collective-permute-done.6 = bf16[16,32,1024]{2,1,0:T(8,128)(2,1)} collective-permute-done((bf16[16,32,1024]{2,1,0:T(8,128)(2,1)}, bf16[16,32,1024]{2,1,0:T(8,128)(2,1)}, u32[]{:S(2)}, u32[]{:S(2)}) %collective-permute-start.6) | collective-permute-done | bytes 1048608 | tf_op jit(solution)/shard_map/ppermute | solution.py:487
  224.5 1.5 collective-permute-start.9
  226.7 9.1 %turned.1.w_hbm = bf16[896,4096]{1,0:T(8,128)(2,1)} custom-call(bf16[896,4096]{1,0:T(8,128)(2,1)} %bitcast.65), custom_call_target="tpu_custom_call" | custom-call | flops 3000000000 | bytes 1048576 | tf_op jit(solution)/shard_map/turned/pallas_call | solution.py:338
  235.8 1.9 slice.92
  237.7 1.9 slice.93
  239.5 7.3 %collective-permute-done.12 = bf16[16,32,1024]{2,1,0:T(8,128)(2,1)S(1)} collective-permute-done((bf16[16,32,1024]{2,1,0:T(8,128)(2,1)S(1)}, bf16[16,32,1024]{2,1,0:T(8,128)(2,1)S(1)}, u32[]{:S(2)}, u32[]{:S(2)}) %collective-permute-start.12) | collective-permute-done | bytes 1048608 | tf_op jit(solution)/shard_map/ppermute | solution.py:487
  246.9 2.7 collective-permute-start.17
  250.1 2.3 pad_maximum_fusion
  252.4 8.3 %all-to-all-start.9 = ((bf16[16,128,256]{2,1,0:T(8,128)(2,1)}), bf16[16,128,256]{2,1,0:T(8,128)(2,1)S(1)}, u32[]{:S(2)}, u32[]{:S(2)}) async-start(bf16[16,128,256]{2,1,0:T(8,128)(2,1)} %bitcast.48), calls=%async_computation.9 | async-start | bytes 2097152 | tf_op jit(solution)/shard_map/all_to_all | solution.py:483
  261.5 1.6 reshape.168.gates
  264.2 1.9 slice.91
  266.3 2.7 collective-permute-start.15
  269.0 18.2 %collective-permute-done.9 = bf16[16,32,1024]{2,1,0:T(8,128)(2,1)} collective-permute-done((bf16[16,32,1024]{2,1,0:T(8,128)(2,1)}, bf16[16,32,1024]{2,1,0:T(8,128)(2,1)}, u32[]{:S(2)}, u32[]{:S(2)}) %collective-permute-start.9) | collective-permute-done | bytes 1048608 | tf_op jit(solution)/shard_map/ppermute | solution.py:491
  287.2 1.2 collective-permute-start.2
  288.4 17.2 %expert_grads.4 = (bf16[2,4,2,128,2,896]{5,4,3,2,1,0:T(2,128)(2,1)}, f32[8,512]{1,0:T(8,128)}) custom-call(s32[2]{0:T(128)} %pad_add_fusion.1.at_ref, bf16[4,4,2,16,1024]{4,3,2,1,0:T(8,128)(2,1)} %bitcast.74, bf16[4,4,2,16,1024]{4,3,2,1,0:T(8,128)(2,1)} %bitcast.33.left, bf16[4,4,2,16,1024]{4,3,2,1,0:T(8,128)(2,1)} %bitcast.34.right, ...), custom_call_target="tpu_custom_call" | custom-call | flops 6000000000 | bytes 1048576 | tf_op jit(solution)/shard_map/expert_grads/pallas_call | solution.py:448
  306.5 1.9 slice.89
  308.7 2.4 collective-permute-start.11
  311.1 17.2 %expert_grads.5 = (bf16[2,4,2,128,2,896]{5,4,3,2,1,0:T(2,128)(2,1)}, f32[8,512]{1,0:T(8,128)}) custom-call(s32[2]{0:T(128)} %pad_add_fusion.1.at_ref, bf16[4,4,2,16,1024]{4,3,2,1,0:T(8,128)(2,1)} %bitcast.66, bf16[4,4,2,16,1024]{4,3,2,1,0:T(8,128)(2,1)} %bitcast.68, bf16[4,4,2,16,1024]{4,3,2,1,0:T(8,128)(2,1)} %bitcast.29.right, ...), custom_call_target="tpu_custom_call", output_to_operand_aliasing={{0}: (9, {})} | custom-call | flops 6000000000 | bytes 1048576 | tf_op jit(solution)/shard_map/expert_grads/pallas_call | solution.py:448
  330.9 2.5 collective-permute-start.4
  334.8 17.2 %expert_grads.6 = (bf16[2,4,2,128,2,896]{5,4,3,2,1,0:T(2,128)(2,1)}, f32[8,512]{1,0:T(8,128)}) custom-call(s32[2]{0:T(128)} %pad_add_fusion.at_ref, bf16[4,4,2,16,1024]{4,3,2,1,0:T(8,128)(2,1)} %bitcast.73, bf16[4,4,2,16,1024]{4,3,2,1,0:T(8,128)(2,1)} %bitcast.67, bf16[4,4,2,16,1024]{4,3,2,1,0:T(8,128)(2,1)} %bitcast.23.right, ...), custom_call_target="tpu_custom_call", output_to_operand_aliasing={{0}: (9, {})} | custom-call | flops 6000000000 | bytes 1048576 | tf_op jit(solution)/shard_map/expert_grads/pallas_call | solution.py:448
  353.0 17.2 %expert_grads.7 = (bf16[2,4,2,128,2,896]{5,4,3,2,1,0:T(2,128)(2,1)}, f32[8,512]{1,0:T(8,128)}) custom-call(s32[2]{0:T(128)} %pad_add_fusion.at_ref, bf16[4,4,2,16,1024]{4,3,2,1,0:T(8,128)(2,1)} %bitcast.10.own, bf16[4,4,2,16,1024]{4,3,2,1,0:T(8,128)(2,1)} %bitcast.69, bf16[4,4,2,16,1024]{4,3,2,1,0:T(8,128)(2,1)} %bitcast.70, ...), custom_call_target="tpu_custom_call", output_to_operand_aliasing={{0}: (9, {})} | custom-call | flops 6000000000 | bytes 1048576 | tf_op jit(solution)/shard_map/expert_grads/pallas_call | solution.py:448
  372.2 3.3 all-to-all-start.7
  375.7 4.8 %all-to-all-done.7 = f32[8,1,256]{2,1,0:T(1,128)S(1)} async-done(((f32[8,1,256]{2,1,0:T(1,128)}), f32[8,1,256]{2,1,0:T(1,128)S(1)}, u32[]{:S(2)}, u32[]{:S(2)}) %all-to-all-start.7) | async-done | bytes 8224 | tf_op jit(solution)/shard_map/all_to_all | solution.py:483
  381.3 10.2 %all-to-all-start.8 = ((f32[16,1,16]{2,1,0:T(1,128)}), f32[16,1,16]{2,1,0:T(1,128)S(1)}, u32[]{:S(2)}, u32[]{:S(2)}) async-start(f32[16,1,16]{2,1,0:T(1,128)} %all_to_all.52), calls=%async_computation.8 | async-start | bytes 16384 | tf_op jit(solution)/shard_map/all_to_all | solution.py:483
  392.2 6.4 %all-to-all-done.8 = f32[16,1,16]{2,1,0:T(1,128)S(1)} async-done(((f32[16,1,16]{2,1,0:T(1,128)}), f32[16,1,16]{2,1,0:T(1,128)S(1)}, u32[]{:S(2)}, u32[]{:S(2)}) %all-to-all-start.8) | async-done | bytes 1056 | tf_op jit(solution)/shard_map/all_to_all | solution.py:483
  (111 shorter events, 23.3 us)
Async XLA Ops:
  7.2 129.9 %all-gather.2.cloned.1.call-start = ((), (), s32[]{:S(2)}) async-start(), calls=%async_computation.10 | async-start | bytes 8650752 | tf_op jit(solution)/shard_map/all_gather | solution.py:512
  11.4 29.4 %copy-start.19 = (f32[4]{0:T(128)S(1)}, f32[4]{0:T(128)}, u32[]{:S(2)}) copy-start(f32[4]{0:T(128)} %param.23) | copy-start | bytes 52
  41.4 16.4 %copy-start.18 = (bf16[16,16]{1,0:T(8,128)(2,1)S(1)}, bf16[16,16]{1,0:T(8,128)(2,1)}, u32[]{:S(2)}) copy-start(bf16[16,16]{1,0:T(8,128)(2,1)} %get-tuple-element.41) | copy-start | bytes 1540
  57.0 6.7 %copy-start.20 = (f32[4]{0:T(128)S(1)}, f32[4]{0:T(128)}, u32[]{:S(2)}) copy-start(f32[4]{0:T(128)} %param.24) | copy-start | bytes 52
  59.6 16.7 %all-to-all-start.1 = ((bf16[8,288,128]{2,1,0:T(8,128)(2,1)}), bf16[8,288,128]{2,1,0:T(8,128)(2,1)S(1)}, u32[]{:S(2)}, u32[]{:S(2)}) async-start(bf16[8,288,128]{2,1,0:T(8,128)(2,1)} %pad_maximum_fusion.1), calls=%async_computation.1 | async-start | bytes 1179648 | tf_op jit(solution)/shard_map/all_to_all | solution.py:483
  76.3 7.1 %copy-start.9 = (bf16[8,288,128]{2,1,0:T(8,128)(2,1)}, bf16[8,288,128]{2,1,0:T(8,128)(2,1)S(1)}, u32[]{:S(2)}) copy-start(bf16[8,288,128]{2,1,0:T(8,128)(2,1)S(1)} %all-to-all-done.1.packs_ref) | copy-start | bytes 1769476
  77.1 16.7 %all-to-all-start.4 = ((bf16[16,1,128]{2,1,0:T(2,128)(2,1)}), bf16[16,1,128]{2,1,0:T(2,128)(2,1)S(1)}, u32[]{:S(2)}, u32[]{:S(2)}) async-start(bf16[16,1,128]{2,1,0:T(2,128)(2,1)} %all_to_all.55), calls=%async_computation.4 | async-start | bytes 16384 | tf_op jit(solution)/shard_map/all_to_all | solution.py:483
  93.8 35.7 %all-to-all-start.5 = ((bf16[16,256,256]{2,1,0:T(8,128)(2,1)}), bf16[16,256,256]{2,1,0:T(8,128)(2,1)S(1)}, u32[]{:S(2)}, u32[]{:S(2)}) async-start(bf16[16,256,256]{2,1,0:T(8,128)(2,1)} %bitcast.71), calls=%async_computation.5 | async-start | bytes 4194304 | tf_op jit(solution)/shard_map/all_to_all | solution.py:483
  129.5 36.1 %all-to-all-start.2 = ((bf16[16,256,256]{2,1,0:T(8,128)(2,1)}), bf16[16,256,256]{2,1,0:T(8,128)(2,1)}, u32[]{:S(2)}, u32[]{:S(2)}) async-start(bf16[16,256,256]{2,1,0:T(8,128)(2,1)} %bitcast.72), calls=%async_computation.2 | async-start | bytes 4194304 | tf_op jit(solution)/shard_map/all_to_all | solution.py:483
  143.6 1.0 copy-start
  165.5 24.0 %all-to-all-start.6 = ((bf16[16,32,1024]{2,1,0:T(8,128)(2,1)}), bf16[16,32,1024]{2,1,0:T(8,128)(2,1)S(1)}, u32[]{:S(2)}, u32[]{:S(2)}) async-start(bf16[16,32,1024]{2,1,0:T(8,128)(2,1)} %bitcast.57), calls=%async_computation.6 | async-start | bytes 2097152 | tf_op jit(solution)/shard_map/all_to_all | solution.py:483
  189.5 1.0 copy-start.7
  190.5 21.6 %all-to-all-start.3 = ((bf16[16,32,1024]{2,1,0:T(8,128)(2,1)}), bf16[16,32,1024]{2,1,0:T(8,128)(2,1)S(1)}, u32[]{:S(2)}, u32[]{:S(2)}) async-start(bf16[16,32,1024]{2,1,0:T(8,128)(2,1)} %bitcast.9), calls=%async_computation.3 | async-start | bytes 2097152 | tf_op jit(solution)/shard_map/all_to_all | solution.py:483
  195.0 29.5 %collective-permute-start.6 = (bf16[16,32,1024]{2,1,0:T(8,128)(2,1)}, bf16[16,32,1024]{2,1,0:T(8,128)(2,1)}, u32[]{:S(2)}, u32[]{:S(2)}) collective-permute-start(bf16[16,32,1024]{2,1,0:T(8,128)(2,1)} %copy-done.7), channel_id=1, source_target_pairs={{0,16},{16,32},{32,48},{48,0},{1,17},{17,33},{33,49},{49,1},{2,18}... | collective-permute-start | bytes 3145736 | tf_op jit(solution)/shard_map/ppermute | solution.py:487
  198.8 25.7 %collective-permute-start.8 = (bf16[16,32,1024]{2,1,0:T(8,128)(2,1)}, bf16[16,32,1024]{2,1,0:T(8,128)(2,1)}, u32[]{:S(2)}, u32[]{:S(2)}) collective-permute-start(bf16[16,32,1024]{2,1,0:T(8,128)(2,1)} %copy-done.7), channel_id=1, source_target_pairs={{0,48},{16,0},{32,16},{48,32},{1,49},{17,1},{33,17},{49,33},{2,50}... | collective-permute-start | bytes 3145736 | tf_op jit(solution)/shard_map/ppermute | solution.py:487
  212.2 23.6 %copy-start.1 = (bf16[16,32,1024]{2,1,0:T(8,128)(2,1)}, bf16[16,32,1024]{2,1,0:T(8,128)(2,1)S(1)}, u32[]{:S(2)}) copy-start(bf16[16,32,1024]{2,1,0:T(8,128)(2,1)S(1)} %all-to-all-done.3) | copy-start | bytes 3145732
  212.2 34.7 %collective-permute-start.12 = (bf16[16,32,1024]{2,1,0:T(8,128)(2,1)S(1)}, bf16[16,32,1024]{2,1,0:T(8,128)(2,1)S(1)}, u32[]{:S(2)}, u32[]{:S(2)}) collective-permute-start(bf16[16,32,1024]{2,1,0:T(8,128)(2,1)S(1)} %all-to-all-done.3), channel_id=1, source_target_pairs={{0,16},{16,32},{32,48},{48,0},{1,17},{17,33},{33,49},{49,1},{2,18}... | collective-permute-start | bytes 3145736 | tf_op jit(solution)/shard_map/ppermute | solution.py:487
  216.0 30.9 %collective-permute-start.13 = (bf16[16,32,1024]{2,1,0:T(8,128)(2,1)S(1)}, bf16[16,32,1024]{2,1,0:T(8,128)(2,1)}, u32[]{:S(2)}, u32[]{:S(2)}) collective-permute-start(bf16[16,32,1024]{2,1,0:T(8,128)(2,1)S(1)} %all-to-all-done.3), channel_id=1, source_target_pairs={{0,48},{16,0},{32,16},{48,32},{1,49},{17,1},{33,17},{49,33},{2,50}... | collective-permute-start | bytes 3145736 | tf_op jit(solution)/shard_map/ppermute | solution.py:487
  218.8 47.3 %collective-permute-start = (bf16[16,32,1024]{2,1,0:T(8,128)(2,1)S(1)}, bf16[16,32,1024]{2,1,0:T(8,128)(2,1)}, u32[]{:S(2)}, u32[]{:S(2)}) collective-permute-start(bf16[16,32,1024]{2,1,0:T(8,128)(2,1)S(1)} %all-to-all-done.3), channel_id=1, source_target_pairs={{0,64},{64,0},{1,65},{65,1},{2,66},{66,2},{3,67},{67,3},{4,68},{68... | collective-permute-start | bytes 3145736 | tf_op jit(solution)/shard_map/ppermute | solution.py:491
  224.5 44.5 %collective-permute-start.7 = (bf16[16,32,1024]{2,1,0:T(8,128)(2,1)}, bf16[16,32,1024]{2,1,0:T(8,128)(2,1)S(1)}, u32[]{:S(2)}, u32[]{:S(2)}) collective-permute-start(bf16[16,32,1024]{2,1,0:T(8,128)(2,1)} %collective-permute-done.6), channel_id=1, source_target_pairs={{0,64},{64,0},{1,65},{65,1},{2,66},{66,2},{3,67},{67,3},{4,68},{68... | collective-permute-start | bytes 3145736 | tf_op jit(solution)/shard_map/ppermute | solution.py:491
  224.5 62.8 %collective-permute-start.9 = (bf16[16,32,1024]{2,1,0:T(8,128)(2,1)}, bf16[16,32,1024]{2,1,0:T(8,128)(2,1)}, u32[]{:S(2)}, u32[]{:S(2)}) collective-permute-start(bf16[16,32,1024]{2,1,0:T(8,128)(2,1)} %collective-permute-done.8), channel_id=1, source_target_pairs={{0,64},{64,0},{1,65},{65,1},{2,66},{66,2},{3,67},{67,3},{4,68},{68... | collective-permute-start | bytes 3145736 | tf_op jit(solution)/shard_map/ppermute | solution.py:491
  246.8 5.5 %copy-start.3 = (bf16[16,32,1024]{2,1,0:T(8,128)(2,1)}, bf16[16,32,1024]{2,1,0:T(8,128)(2,1)S(1)}, u32[]{:S(2)}) copy-start(bf16[16,32,1024]{2,1,0:T(8,128)(2,1)S(1)} %collective-permute-done.12) | copy-start | bytes 3145732
  246.8 19.2 %collective-permute-start.16 = (bf16[8,32,1024]{2,1,0:T(8,128)(2,1)}, bf16[8,32,1024]{2,1,0:T(8,128)(2,1)}, u32[]{:S(2)}, u32[]{:S(2)}) collective-permute-start(bf16[8,32,1024]{2,1,0:T(8,128)(2,1)} %slice.92), channel_id=1, source_target_pairs={{0,16},{16,32},{32,48},{48,0},{1,17},{17,33},{33,49},{49,1},{2,18}... | collective-permute-start | bytes 1572872 | tf_op jit(solution)/shard_map/ppermute | solution.py:487
  246.9 19.5 %collective-permute-start.17 = (bf16[8,32,1024]{2,1,0:T(8,128)(2,1)}, bf16[8,32,1024]{2,1,0:T(8,128)(2,1)}, u32[]{:S(2)}, u32[]{:S(2)}) collective-permute-start(bf16[8,32,1024]{2,1,0:T(8,128)(2,1)} %slice.93), channel_id=1, source_target_pairs={{0,48},{16,0},{32,16},{48,32},{1,49},{17,1},{33,17},{49,33},{2,50}... | collective-permute-start | bytes 1572872 | tf_op jit(solution)/shard_map/ppermute | solution.py:487
  250.1 10.6 %copy-start.16 = (f32[4,1024]{1,0:T(4,128)S(1)}, f32[4,1024]{1,0:T(4,128)}, u32[]{:S(2)}) copy-start(f32[4,1024]{1,0:T(4,128)} %get-tuple-element.58) | copy-start | bytes 49156
  250.1 10.6 %copy-start.17 = (f32[4,1024]{1,0:T(4,128)S(1)}, f32[4,1024]{1,0:T(4,128)}, u32[]{:S(2)}) copy-start(f32[4,1024]{1,0:T(4,128)} %get-tuple-element.57) | copy-start | bytes 49156
  252.4 119.9 %all-to-all-start.9 = ((bf16[16,128,256]{2,1,0:T(8,128)(2,1)}), bf16[16,128,256]{2,1,0:T(8,128)(2,1)S(1)}, u32[]{:S(2)}, u32[]{:S(2)}) async-start(bf16[16,128,256]{2,1,0:T(8,128)(2,1)} %bitcast.48), calls=%async_computation.9 | async-start | bytes 2097152 | tf_op jit(solution)/shard_map/all_to_all | solution.py:483
  263.0 3.0 copy-start.8
  266.1 67.4 %collective-permute-start.5 = (bf16[16,32,1024]{2,1,0:T(8,128)(2,1)S(1)}, bf16[16,32,1024]{2,1,0:T(8,128)(2,1)S(1)}, u32[]{:S(2)}, u32[]{:S(2)}) collective-permute-start(bf16[16,32,1024]{2,1,0:T(8,128)(2,1)S(1)} %copy-done.8), channel_id=1, source_target_pairs={{0,64},{64,0},{1,65},{65,1},{2,66},{66,2},{3,67},{67,3},{4,68},{68... | collective-permute-start | bytes 3145736 | tf_op jit(solution)/shard_map/ppermute | solution.py:491
  266.1 42.3 %collective-permute-start.14 = (bf16[8,32,1024]{2,1,0:T(8,128)(2,1)S(1)}, bf16[8,32,1024]{2,1,0:T(8,128)(2,1)S(1)}, u32[]{:S(2)}, u32[]{:S(2)}) collective-permute-start(bf16[8,32,1024]{2,1,0:T(8,128)(2,1)S(1)} %slice.90), channel_id=1, source_target_pairs={{0,16},{16,32},{32,48},{48,0},{1,17},{17,33},{33,49},{49,1},{2,18}... | collective-permute-start | bytes 1572872 | tf_op jit(solution)/shard_map/ppermute | solution.py:487
  266.3 42.3 %collective-permute-start.15 = (bf16[8,32,1024]{2,1,0:T(8,128)(2,1)}, bf16[8,32,1024]{2,1,0:T(8,128)(2,1)S(1)}, u32[]{:S(2)}, u32[]{:S(2)}) collective-permute-start(bf16[8,32,1024]{2,1,0:T(8,128)(2,1)} %slice.91), channel_id=1, source_target_pairs={{0,48},{16,0},{32,16},{48,32},{1,49},{17,1},{33,17},{49,33},{2,50}... | collective-permute-start | bytes 1572872 | tf_op jit(solution)/shard_map/ppermute | solution.py:487
  269.0 36.6 %copy-start.2 = (bf16[16,32,1024]{2,1,0:T(8,128)(2,1)}, bf16[16,32,1024]{2,1,0:T(8,128)(2,1)S(1)}, u32[]{:S(2)}) copy-start(bf16[16,32,1024]{2,1,0:T(8,128)(2,1)S(1)} %collective-permute-done.7) | copy-start | bytes 3145732
  269.0 60.7 %collective-permute-start.1 = (bf16[16,32,1024]{2,1,0:T(8,128)(2,1)}, bf16[16,32,1024]{2,1,0:T(8,128)(2,1)S(1)}, u32[]{:S(2)}, u32[]{:S(2)}) collective-permute-start(bf16[16,32,1024]{2,1,0:T(8,128)(2,1)} %collective-permute-done), channel_id=1, source_target_pairs={{0,16},{16,32},{32,48},{48,0},{1,17},{17,33},{33,49},{49,1},{2,18}... | collective-permute-start | bytes 3145736 | tf_op jit(solution)/shard_map/ppermute | solution.py:487
  287.2 42.6 %collective-permute-start.2 = (bf16[16,32,1024]{2,1,0:T(8,128)(2,1)}, bf16[16,32,1024]{2,1,0:T(8,128)(2,1)S(1)}, u32[]{:S(2)}, u32[]{:S(2)}) collective-permute-start(bf16[16,32,1024]{2,1,0:T(8,128)(2,1)} %collective-permute-done), channel_id=1, source_target_pairs={{0,48},{16,0},{32,16},{48,32},{1,49},{17,1},{33,17},{49,33},{2,50}... | collective-permute-start | bytes 3145736 | tf_op jit(solution)/shard_map/ppermute | solution.py:487
  308.4 2.7 copy-start.11
  308.4 25.0 %collective-permute-start.10 = (bf16[8,32,1024]{2,1,0:T(8,128)(2,1)}, bf16[8,32,1024]{2,1,0:T(8,128)(2,1)S(1)}, u32[]{:S(2)}, u32[]{:S(2)}) collective-permute-start(bf16[8,32,1024]{2,1,0:T(8,128)(2,1)} %slice.88), channel_id=1, source_target_pairs={{0,16},{16,32},{32,48},{48,0},{1,17},{17,33},{33,49},{49,1},{2,18}... | collective-permute-start | bytes 1572872 | tf_op jit(solution)/shard_map/ppermute | solution.py:487
  308.7 2.4 copy-start.13
  308.7 24.8 %collective-permute-start.11 = (bf16[8,32,1024]{2,1,0:T(8,128)(2,1)}, bf16[8,32,1024]{2,1,0:T(8,128)(2,1)S(1)}, u32[]{:S(2)}, u32[]{:S(2)}) collective-permute-start(bf16[8,32,1024]{2,1,0:T(8,128)(2,1)} %slice.89), channel_id=1, source_target_pairs={{0,48},{16,0},{32,16},{48,32},{1,49},{17,1},{33,17},{49,33},{2,50}... | collective-permute-start | bytes 1572872 | tf_op jit(solution)/shard_map/ppermute | solution.py:487
  329.7 22.3 %copy-start.4 = (bf16[16,32,1024]{2,1,0:T(8,128)(2,1)}, bf16[16,32,1024]{2,1,0:T(8,128)(2,1)S(1)}, u32[]{:S(2)}) copy-start(bf16[16,32,1024]{2,1,0:T(8,128)(2,1)S(1)} %collective-permute-done.1) | copy-start | bytes 3145732
  329.8 22.2 %collective-permute-start.3 = (bf16[8,32,1024]{2,1,0:T(8,128)(2,1)S(1)}, bf16[8,32,1024]{2,1,0:T(8,128)(2,1)S(1)}, u32[]{:S(2)}, u32[]{:S(2)}) collective-permute-start(bf16[8,32,1024]{2,1,0:T(8,128)(2,1)S(1)} %slice.85), channel_id=1, source_target_pairs={{0,16},{16,32},{32,48},{48,0},{1,17},{17,33},{33,49},{49,1},{2,18}... | collective-permute-start | bytes 1572872 | tf_op jit(solution)/shard_map/ppermute | solution.py:487
  329.9 22.1 %copy-start.5 = (bf16[16,32,1024]{2,1,0:T(8,128)(2,1)}, bf16[16,32,1024]{2,1,0:T(8,128)(2,1)S(1)}, u32[]{:S(2)}) copy-start(bf16[16,32,1024]{2,1,0:T(8,128)(2,1)S(1)} %collective-permute-done.2) | copy-start | bytes 3145732
  330.9 21.1 %collective-permute-start.4 = (bf16[8,32,1024]{2,1,0:T(8,128)(2,1)}, bf16[8,32,1024]{2,1,0:T(8,128)(2,1)S(1)}, u32[]{:S(2)}, u32[]{:S(2)}) collective-permute-start(bf16[8,32,1024]{2,1,0:T(8,128)(2,1)} %slice.86), channel_id=1, source_target_pairs={{0,48},{16,0},{32,16},{48,32},{1,49},{17,1},{33,17},{49,33},{2,50}... | collective-permute-start | bytes 1572872 | tf_op jit(solution)/shard_map/ppermute | solution.py:487
  333.4 1.0 copy-start.6
  333.4 1.2 copy-start.10
  333.4 1.3 copy-start.12
  352.0 1.0 copy-start.15
  372.2 8.3 %all-to-all-start.7 = ((f32[8,1,256]{2,1,0:T(1,128)}), f32[8,1,256]{2,1,0:T(1,128)S(1)}, u32[]{:S(2)}, u32[]{:S(2)}) async-start(f32[8,1,256]{2,1,0:T(1,128)} %all_to_all.50), calls=%async_computation.7 | async-start | bytes 16384 | tf_op jit(solution)/shard_map/all_to_all | solution.py:483
  381.3 17.3 %all-to-all-start.8 = ((f32[16,1,16]{2,1,0:T(1,128)}), f32[16,1,16]{2,1,0:T(1,128)S(1)}, u32[]{:S(2)}, u32[]{:S(2)}) async-start(f32[16,1,16]{2,1,0:T(1,128)} %all_to_all.52), calls=%async_computation.8 | async-start | bytes 16384 | tf_op jit(solution)/shard_map/all_to_all | solution.py:483
  (1 other events, 0.8 us)
Sparse Core Ops, SparseCore 0:
  40.9 73.6 all-gather.1
where the time goes:
time: 410 us; the launch traced here: 407 us
  Pallas kernels  133 us (32%)
  waiting for transfers between devices  114 us (28%)
  starting transfers between devices  84.2 us (21%)
  blocking collectives  28.6 us (7%)
  local copies, waits for them, and re-layouts  27.1 us (7%)
  between operations  14.4 us (4%)
  other arithmetic  6.66 us (2%)
    all_to_all x9, waiting for transfers between devices, a2a(): return lax.all_to_all(array, axis, split_axis=0, concat_axis=0, tiled=True)  82.4 us
    pallas_call x4, Pallas kernels, expert_grads(): pl.pallas_call(functools.partial(expert_kernel, half), in_specs=[pl.Block...  68.8 us
    all_to_all x9, starting transfers between devices, a2a(): return lax.all_to_all(array, axis, split_axis=0, concat_axis=0, tiled=True)  58.7 us
    all_to_all x1, blocking collectives, a2a(): return lax.all_to_all(array, axis, split_axis=0, concat_axis=0, tiled=True)  28.6 us
    ppermute x14, starting transfers between devices, shifted(): return lax.ppermute(array, 'x', [(i, (i + by) % 4) for i in range(4)])  24 us
    pallas_call x2, Pallas kernels, span_grads(): pl.pallas_call(grads_kernel, grid=(spans,), in_specs=[pl.BlockSpec(memory...  20.6 us
    ppermute x4, waiting for transfers between devices, other_row(): return lax.ppermute(array, 'yl', [(0, 1), (1, 0)])  18.2 us
    pallas_call x1, Pallas kernels, local_states(): pl.pallas_call(states_kernel, out_shape=out, scratch_shapes=[pltpu.VMEM((...  15.6 us
  transfers between devices with their start and end apart: 28, of which 10 were waited for; matrix products, arithmetic and copies ran while one was open for 6% of the time, Pallas kernels for 32%

commit v1 on v0

--- a/solution.py
+++ b/solution.py
@@ -491,8 +491,8 @@
     return lax.ppermute(array, "yl", [(0, 1), (1, 0)])
 
 
-def along_x(own):
-    return joined_x((own, shifted(own, 1), shifted(own, -1)))
+def near_x(own):
+    return (own, shifted(own, 1), shifted(own, -1))
 
 
 def joined_x(pieces):
@@ -539,12 +539,18 @@
 
     gate_rows = gate_rows.reshape(16, 8, 16).transpose(1, 0, 2)
     gate_rows = gate_rows.astype(F32).reshape(2, 4, 2, 128, 1)
-    near = (arrived[1], shifted(arrived[1], 1), shifted(arrived[1], -1))
+    near = near_x(arrived[1])
     across = other_row(arrived[1])
     mine = joined_x(near)
-    theirs = joined_x((across, other_row(near[1]), other_row(near[2])))
+    cross_left = other_row(near[1])
+    cross_right = other_row(near[2])
+    theirs = joined_x((across, cross_left, cross_right))
     partner = other_row(arrived[0])
-    sets = [(1, 0, mine), (0, 0, along_x(arrived[0])), (1, 1, theirs), (0, 1, along_x(partner))]
+    local = near_x(arrived[0])
+    local = joined_x(local)
+    partner = near_x(partner)
+    partner = joined_x(partner)
+    sets = [(1, 0, mine), (0, 0, local), (1, 1, theirs), (0, 1, partner)]
 
     x_at, y_at = lax.axis_index("x"), lax.axis_index("yl")
     saved = saved_pre.reshape(2, 4, 2, 128, 2, 896)
@@ -558,15 +564,17 @@
     ]
     low, high = [jnp.where(y_at == 0, a, b) for a, b in ((first, second), (second, first))]
     partial = jnp.concatenate([low, high], axis=0)
-    summed = jnp.sum(a2a(partial, SEQ), axis=0)
-    totals = a2a(summed.reshape(16, 16), EXP).reshape(256, 1)
+    both = jnp.concatenate([grads[0][0], grads[1][0]], axis=0).reshape(16, 128, 2 * NST)
+    both = a2a(both, EXP)
+    partial, both = lax.optimization_barrier((partial, both))
+    totals = a2a(partial.reshape(128, 16), BOTH).reshape(8, 16, 16)
+    totals = jnp.sum(totals, axis=0).reshape(256, 1)
     slot = lax.broadcasted_iota(jnp.int32, (256, 128), 0)
     route_grads = jnp.stack(
         [jnp.sum(jnp.where(slot == targets[k], totals, 0.0), axis=0) for k in range(2)], axis=1
     )
 
-    both = jnp.concatenate([grads[0][0], grads[1][0]], axis=0).reshape(16, 128, 2 * NST)
-    both = jnp.sum(a2a(both, EXP).astype(F32), axis=0)
+    both = jnp.sum(both.astype(F32), axis=0)
     step_grads = jnp.concatenate([grads[0][1], grads[1][1]], axis=1)
     pre_grads = out.reshape(1, 2048, 2, 896)
     return (pre_grads, route_grads, both[:, :NST], both[:, NST:], step_grads)

time: 410 us -> 402 us (0.980)
    all_to_all x9 -> x8, starting transfers between devices: 58.7 us -> 54.4 us  [a2a(): return lax.all_to_all(array, axis, split_axis=0, concat_axis=0, tiled=True)]
    all_to_all x9 -> x8, waiting for transfers between devices: 82.4 us -> 79.8 us  [a2a(): return lax.all_to_all(array, axis, split_axis=0, concat_axis=0, tiled=True)]
  transfers between devices with their start and end apart: 28 -> 27, of which waited for: 10 -> 9; matrix products, arithmetic and copies ran while one was open for 6% -> 6% of each run, Pallas kernels for 32% -> 32%
where the time goes in v1:
time: 402 us; the launch traced here: 399 us
  Pallas kernels  133 us (33%)
  waiting for transfers between devices  111 us (28%)
  starting transfers between devices  80.5 us (20%)
  blocking collectives  28.6 us (7%)
  local copies, waits for them, and re-layouts  26.1 us (6%)
  between operations  14.4 us (4%)
  other arithmetic  5.87 us (1%)
    all_to_all x8, waiting for transfers between devices, a2a(): return lax.all_to_all(array, axis, split_axis=0, concat_axis=0, tiled=True)  79.8 us
    pallas_call x4, Pallas kernels, expert_grads(): pl.pallas_call(functools.partial(expert_kernel, half), in_specs=[pl.Block...  68.8 us
    all_to_all x8, starting transfers between devices, a2a(): return lax.all_to_all(array, axis, split_axis=0, concat_axis=0, tiled=True)  54.4 us
    all_to_all x1, blocking collectives, a2a(): return lax.all_to_all(array, axis, split_axis=0, concat_axis=0, tiled=True)  28.6 us
    ppermute x14, starting transfers between devices, shifted(): return lax.ppermute(array, 'x', [(i, (i + by) % 4) for i in range(4)])  24.5 us
    pallas_call x2, Pallas kernels, span_grads(): pl.pallas_call(grads_kernel, grid=(spans,), in_specs=[pl.BlockSpec(memory...  20.7 us
    ppermute x4, waiting for transfers between devices, other_row(): return lax.ppermute(array, 'yl', [(0, 1), (1, 0)])  18.1 us
    pallas_call x1, Pallas kernels, local_states(): pl.pallas_call(states_kernel, out_shape=out, scratch_shapes=[pltpu.VMEM((...  15.6 us
  transfers between devices with their start and end apart: 27, of which 9 were waited for; matrix products, arithmetic and copies ran while one was open for 6% of the time, Pallas kernels for 32%

profile of v1, /device:TPU:1, one launch (start us, length us, event | category | flops | bytes accessed | tf_op | source)
XLA Modules:
  0.0 399.3 jit_solution(11811864632875153092)
XLA Ops:
  7.2 1.6 routing.1
  8.8 2.6 first_exchange.1
  11.4 28.6 %all_to_all.57.res_ref = bf16[4,176,1024]{2,1,0:T(8,128)(2,1)S(1)} all-to-all(bf16[4,176,1024]{2,1,0:T(8,128)(2,1)} %first_exchange.1), channel_id=1, replica_groups=mesh['yl'=2,'x'=4,'yh'=2,'zh'=2,'zl'=2,'core'=2] {'yh','zh'}, dimensions={0} | all-to-all | bytes 2883584 | tf_op jit(solution)/shard_map/all_to_all | solution.py:483
  41.4 15.6 %states.1 = (f32[16,8,128]{2,1,0:T(8,128)}, f32[16,128,8]{2,1,0:T(8,128)}, bf16[16,256,128]{2,1,0:T(8,128)(2,1)}, bf16[16,256,128]{2,1,0:T(8,128)(2,1)}, f32[16,...) custom-call(bf16[2048,256]{1,0:T(8,128)(2,1)} %x_ref.5, bf16[2048,256]{1,0:T(8,128)(2,1)} %g_ref.5, ...), custom_call_target="tpu_custom_call" | custom-call | flops 8000000000 | bytes 1048576 | tf_op jit(solution)/shard_map/states/pallas_call | solution.py:102
  59.6 4.1 %all-to-all-start.1 = ((bf16[8,288,128]{2,1,0:T(8,128)(2,1)}), bf16[8,288,128]{2,1,0:T(8,128)(2,1)S(1)}, u32[]{:S(2)}, u32[]{:S(2)}) async-start(bf16[8,288,128]{2,1,0:T(8,128)(2,1)} %pad_maximum_fusion.1), calls=%async_computation.1 | async-start | bytes 1179648 | tf_op jit(solution)/shard_map/all_to_all | solution.py:483
  64.4 11.7 %all-to-all-done.1.packs_ref = bf16[8,288,128]{2,1,0:T(8,128)(2,1)S(1)} async-done(((bf16[8,288,128]{2,1,0:T(8,128)(2,1)}), bf16[8,288,128]{2,1,0:T(8,128)(2,1)S(1)}, u32[]{:S(2)}, u32[]{:S(2)}) %all-to-all-start.1) | async-done | bytes 589856 | tf_op jit(solution)/shard_map/all_to_all | solution.py:483
  76.9 6.4 %all-to-all-start.4 = ((bf16[16,1,128]{2,1,0:T(2,128)(2,1)}), bf16[16,1,128]{2,1,0:T(2,128)(2,1)S(1)}, u32[]{:S(2)}, u32[]{:S(2)}) async-start(bf16[16,1,128]{2,1,0:T(2,128)(2,1)} %all_to_all.47), calls=%async_computation.4 | async-start | bytes 16384 | tf_op jit(solution)/shard_map/all_to_all | solution.py:483
  83.3 10.4 %span_grads.3 = (bf16[4,4,2,128,256]{4,3,2,1,0:T(8,128)(2,1)}, bf16[1024,256]{1,0:T(8,128)(2,1)}, f32[4,1024]{1,0:T(4,128)}) custom-call(s32[1]{0:T(128)} %bitcast.2.me_ref, bf16[2048,256]{1,0:T(8,128)(2,1)} %x_ref.5, bf16[2048,256]{1,0:T(8,128)(2,1)} %g_ref.5, bf16[2048,128]{1,0:T(8,128)(2,1)} %b_ref.5, bf16[2048,128]{1,0:T(8,128)(2,1)} %c_ref.5, ...), custom_call_target="tpu_custom_call" | custom-call | flops 5000000000 | bytes 1048576 | tf_op jit(solution)/shard_map/span_grads/pallas_call | solution.py:208
  93.7 7.3 %all-to-all-start.5 = ((bf16[16,256,256]{2,1,0:T(8,128)(2,1)}), bf16[16,256,256]{2,1,0:T(8,128)(2,1)S(1)}, u32[]{:S(2)}, u32[]{:S(2)}) async-start(bf16[16,256,256]{2,1,0:T(8,128)(2,1)} %bitcast.75), calls=%async_computation.5 | async-start | bytes 4194304 | tf_op jit(solution)/shard_map/all_to_all | solution.py:483
  101.0 10.3 %span_grads.2 = (bf16[4,4,2,128,256]{4,3,2,1,0:T(8,128)(2,1)}, bf16[1024,256]{1,0:T(8,128)(2,1)}, f32[4,1024]{1,0:T(4,128)}) custom-call(s32[1]{0:T(128)} %bitcast.2.me_ref, bf16[2048,256]{1,0:T(8,128)(2,1)} %x_ref.5, bf16[2048,256]{1,0:T(8,128)(2,1)} %g_ref.5, bf16[2048,128]{1,0:T(8,128)(2,1)} %b_ref.5, bf16[2048,128]{1,0:T(8,128)(2,1)} %c_ref.5, ...), custom_call_target="tpu_custom_call" | custom-call | flops 5000000000 | bytes 1048576 | tf_op jit(solution)/shard_map/span_grads/pallas_call | solution.py:208
  111.3 18.1 %all-to-all-done.5.x_ref = bf16[16,256,256]{2,1,0:T(8,128)(2,1)S(1)} async-done(((bf16[16,256,256]{2,1,0:T(8,128)(2,1)}), bf16[16,256,256]{2,1,0:T(8,128)(2,1)S(1)}, u32[]{:S(2)}, u32[]{:S(2)}) %all-to-all-start.5) | async-done | bytes 2097184 | tf_op jit(solution)/shard_map/all_to_all | solution.py:483
  129.4 7.6 %all-to-all-start.2 = ((bf16[16,256,256]{2,1,0:T(8,128)(2,1)}), bf16[16,256,256]{2,1,0:T(8,128)(2,1)}, u32[]{:S(2)}, u32[]{:S(2)}) async-start(bf16[16,256,256]{2,1,0:T(8,128)(2,1)} %bitcast.76), calls=%async_computation.2 | async-start | bytes 4194304 | tf_op jit(solution)/shard_map/all_to_all | solution.py:483
  137.0 6.5 %expert_rows.3 = bf16[16,2,16,1024]{3,2,1,0:T(8,128)(2,1)S(1)} custom-call(bf16[16,256,256]{2,1,0:T(8,128)(2,1)S(1)} %all-to-all-done.5.x_ref, bf16[8,4,4,32,1024]{4,3,2,1,0:T(8,128)(2,1)} %bitcast.67, bf16[4,176,1024]{2,1,0:T(8,128)(2,1)S(1)} %all_to_all.57.res_ref), custom_call_target="tpu_custom_call" | custom-call | flops 3000000000 | bytes 1048576 | tf_op jit(solution)/shard_map/expert_rows/pallas_call | solution.py:310
  144.5 20.9 %all-to-all-done.2.x_ref = bf16[16,256,256]{2,1,0:T(8,128)(2,1)} async-done(((bf16[16,256,256]{2,1,0:T(8,128)(2,1)}), bf16[16,256,256]{2,1,0:T(8,128)(2,1)}, u32[]{:S(2)}, u32[]{:S(2)}) %all-to-all-start.2) | async-done | bytes 2097184 | tf_op jit(solution)/shard_map/all_to_all | solution.py:483
  165.4 6.9 %all-to-all-start.6 = ((bf16[16,32,1024]{2,1,0:T(8,128)(2,1)}), bf16[16,32,1024]{2,1,0:T(8,128)(2,1)S(1)}, u32[]{:S(2)}, u32[]{:S(2)}) async-start(bf16[16,32,1024]{2,1,0:T(8,128)(2,1)} %bitcast.61), calls=%async_computation.6 | async-start | bytes 2097152 | tf_op jit(solution)/shard_map/all_to_all | solution.py:483
  172.4 7.9 %expert_rows.2 = bf16[16,2,16,1024]{3,2,1,0:T(8,128)(2,1)} custom-call(bf16[16,256,256]{2,1,0:T(8,128)(2,1)} %all-to-all-done.2.x_ref, bf16[8,4,4,32,1024]{4,3,2,1,0:T(8,128)(2,1)} %bitcast.68, bf16[4,176,1024]{2,1,0:T(8,128)(2,1)S(1)} %all_to_all.57.res_ref), custom_call_target="tpu_custom_call" | custom-call | flops 3000000000 | bytes 1048576 | tf_op jit(solution)/shard_map/expert_rows/pallas_call | solution.py:310
  180.3 9.2 %all-to-all-done.6 = bf16[16,32,1024]{2,1,0:T(8,128)(2,1)S(1)} async-done(((bf16[16,32,1024]{2,1,0:T(8,128)(2,1)}), bf16[16,32,1024]{2,1,0:T(8,128)(2,1)S(1)}, u32[]{:S(2)}, u32[]{:S(2)}) %all-to-all-start.6) | async-done | bytes 1048608 | tf_op jit(solution)/shard_map/all_to_all | solution.py:483
  190.4 4.5 %all-to-all-start.3 = ((bf16[16,32,1024]{2,1,0:T(8,128)(2,1)}), bf16[16,32,1024]{2,1,0:T(8,128)(2,1)S(1)}, u32[]{:S(2)}, u32[]{:S(2)}) async-start(bf16[16,32,1024]{2,1,0:T(8,128)(2,1)} %bitcast.9), calls=%async_computation.3 | async-start | bytes 2097152 | tf_op jit(solution)/shard_map/all_to_all | solution.py:483
  194.9 3.9 collective-permute-start.6
  198.8 2.3 collective-permute-start.8
  201.2 10.9 %all-to-all-done.3 = bf16[16,32,1024]{2,1,0:T(8,128)(2,1)S(1)} async-done(((bf16[16,32,1024]{2,1,0:T(8,128)(2,1)}), bf16[16,32,1024]{2,1,0:T(8,128)(2,1)S(1)}, u32[]{:S(2)}, u32[]{:S(2)}) %all-to-all-start.3) | async-done | bytes 1048608 | tf_op jit(solution)/shard_map/all_to_all | solution.py:483
  212.1 3.9 collective-permute-start.12
  216.0 2.3 collective-permute-start.13
  218.9 5.8 %collective-permute-done.6 = bf16[16,32,1024]{2,1,0:T(8,128)(2,1)} collective-permute-done((bf16[16,32,1024]{2,1,0:T(8,128)(2,1)}, bf16[16,32,1024]{2,1,0:T(8,128)(2,1)}, u32[]{:S(2)}, u32[]{:S(2)}) %collective-permute-start.6) | collective-permute-done | bytes 1048608 | tf_op jit(solution)/shard_map/ppermute | solution.py:487
  224.7 1.5 collective-permute-start.9
  226.9 9.1 %turned.1.w_hbm = bf16[896,4096]{1,0:T(8,128)(2,1)} custom-call(bf16[896,4096]{1,0:T(8,128)(2,1)} %bitcast.69), custom_call_target="tpu_custom_call" | custom-call | flops 3000000000 | bytes 1048576 | tf_op jit(solution)/shard_map/turned/pallas_call | solution.py:338
  236.0 1.9 slice.92
  237.9 1.9 slice.93
  239.7 7.3 %collective-permute-done.12 = bf16[16,32,1024]{2,1,0:T(8,128)(2,1)S(1)} collective-permute-done((bf16[16,32,1024]{2,1,0:T(8,128)(2,1)S(1)}, bf16[16,32,1024]{2,1,0:T(8,128)(2,1)S(1)}, u32[]{:S(2)}, u32[]{:S(2)}) %collective-permute-start.12) | collective-permute-done | bytes 1048608 | tf_op jit(solution)/shard_map/ppermute | solution.py:487
  247.0 2.7 collective-permute-start.17
  250.3 2.3 pad_maximum_fusion
  252.5 8.3 %all-to-all-start.7 = ((bf16[16,128,256]{2,1,0:T(8,128)(2,1)}), bf16[16,128,256]{2,1,0:T(8,128)(2,1)S(1)}, u32[]{:S(2)}, u32[]{:S(2)}) async-start(bf16[16,128,256]{2,1,0:T(8,128)(2,1)} %bitcast.45), calls=%async_computation.7 | async-start | bytes 2097152 | tf_op jit(solution)/shard_map/all_to_all | solution.py:483
  261.6 1.6 reshape.170.gates
  263.2 1.2 slice.90
  264.3 1.9 slice.91
  266.5 2.7 collective-permute-start.15
  269.2 18.1 %collective-permute-done.9 = bf16[16,32,1024]{2,1,0:T(8,128)(2,1)} collective-permute-done((bf16[16,32,1024]{2,1,0:T(8,128)(2,1)}, bf16[16,32,1024]{2,1,0:T(8,128)(2,1)}, u32[]{:S(2)}, u32[]{:S(2)}) %collective-permute-start.9) | collective-permute-done | bytes 1048608 | tf_op jit(solution)/shard_map/ppermute | solution.py:491
  287.3 1.2 collective-permute-start.2
  288.5 17.2 %expert_grads.4 = (bf16[2,4,2,128,2,896]{5,4,3,2,1,0:T(2,128)(2,1)}, f32[8,512]{1,0:T(8,128)}) custom-call(s32[2]{0:T(128)} %pad_add_fusion.1.at_ref, bf16[4,4,2,16,1024]{4,3,2,1,0:T(8,128)(2,1)} %bitcast.78, bf16[4,4,2,16,1024]{4,3,2,1,0:T(8,128)(2,1)} %bitcast.33.left, bf16[4,4,2,16,1024]{4,3,2,1,0:T(8,128)(2,1)} %bitcast.34.right, ...), custom_call_target="tpu_custom_call" | custom-call | flops 6000000000 | bytes 1048576 | tf_op jit(solution)/shard_map/expert_grads/pallas_call | solution.py:448
  306.6 1.9 slice.89
  308.8 2.4 collective-permute-start.11
  311.2 17.2 %expert_grads.5 = (bf16[2,4,2,128,2,896]{5,4,3,2,1,0:T(2,128)(2,1)}, f32[8,512]{1,0:T(8,128)}) custom-call(s32[2]{0:T(128)} %pad_add_fusion.1.at_ref, bf16[4,4,2,16,1024]{4,3,2,1,0:T(8,128)(2,1)} %bitcast.70, bf16[4,4,2,16,1024]{4,3,2,1,0:T(8,128)(2,1)} %bitcast.72, bf16[4,4,2,16,1024]{4,3,2,1,0:T(8,128)(2,1)} %bitcast.29.right, ...), custom_call_target="tpu_custom_call", output_to_operand_aliasing={{0}: (9, {})} | custom-call | flops 6000000000 | bytes 1048576 | tf_op jit(solution)/shard_map/expert_grads/pallas_call | solution.py:448
  330.0 1.0 slice.86
  331.0 2.5 collective-permute-start.4
  334.9 17.2 %expert_grads.6 = (bf16[2,4,2,128,2,896]{5,4,3,2,1,0:T(2,128)(2,1)}, f32[8,512]{1,0:T(8,128)}) custom-call(s32[2]{0:T(128)} %pad_add_fusion.at_ref, bf16[4,4,2,16,1024]{4,3,2,1,0:T(8,128)(2,1)} %bitcast.77, bf16[4,4,2,16,1024]{4,3,2,1,0:T(8,128)(2,1)} %bitcast.71, bf16[4,4,2,16,1024]{4,3,2,1,0:T(8,128)(2,1)} %bitcast.23.right, ...), custom_call_target="tpu_custom_call", output_to_operand_aliasing={{0}: (9, {})} | custom-call | flops 6000000000 | bytes 1048576 | tf_op jit(solution)/shard_map/expert_grads/pallas_call | solution.py:448
  353.1 17.2 %expert_grads.7 = (bf16[2,4,2,128,2,896]{5,4,3,2,1,0:T(2,128)(2,1)}, f32[8,512]{1,0:T(8,128)}) custom-call(s32[2]{0:T(128)} %pad_add_fusion.at_ref, bf16[4,4,2,16,1024]{4,3,2,1,0:T(8,128)(2,1)} %bitcast.10.own, bf16[4,4,2,16,1024]{4,3,2,1,0:T(8,128)(2,1)} %bitcast.73, bf16[4,4,2,16,1024]{4,3,2,1,0:T(8,128)(2,1)} %bitcast.74, ...), custom_call_target="tpu_custom_call", output_to_operand_aliasing={{0}: (9, {})} | custom-call | flops 6000000000 | bytes 1048576 | tf_op jit(solution)/shard_map/expert_grads/pallas_call | solution.py:448
  372.6 9.3 %all-to-all-start.8 = ((f32[128,1,16]{2,1,0:T(1,128)}), f32[128,1,16]{2,1,0:T(1,128)S(1)}, u32[]{:S(2)}, u32[]{:S(2)}) async-start(f32[128,1,16]{2,1,0:T(1,128)} %bitcast.46), calls=%async_computation.8 | async-start | bytes 131072 | tf_op jit(solution)/shard_map/all_to_all | solution.py:483
  382.5 9.1 %all-to-all-done.8 = f32[128,1,16]{2,1,0:T(1,128)S(1)} async-done(((f32[128,1,16]{2,1,0:T(1,128)}), f32[128,1,16]{2,1,0:T(1,128)S(1)}, u32[]{:S(2)}, u32[]{:S(2)}) %all-to-all-start.8) | async-done | bytes 8224 | tf_op jit(solution)/shard_map/all_to_all | solution.py:483
  (106 shorter events, 19.2 us)
Async XLA Ops:
  7.2 129.8 %all-gather.2.cloned.1.call-start = ((), (), s32[]{:S(2)}) async-start(), calls=%async_computation.9 | async-start | bytes 8650752 | tf_op jit(solution)/shard_map/all_gather | solution.py:512
  11.4 29.4 %copy-start.19 = (f32[4]{0:T(128)S(1)}, f32[4]{0:T(128)}, u32[]{:S(2)}) copy-start(f32[4]{0:T(128)} %param.23) | copy-start | bytes 52
  41.4 16.3 %copy-start.18 = (bf16[16,16]{1,0:T(8,128)(2,1)S(1)}, bf16[16,16]{1,0:T(8,128)(2,1)}, u32[]{:S(2)}) copy-start(bf16[16,16]{1,0:T(8,128)(2,1)} %get-tuple-element.43) | copy-start | bytes 1540
  57.0 6.7 %copy-start.20 = (f32[4]{0:T(128)S(1)}, f32[4]{0:T(128)}, u32[]{:S(2)}) copy-start(f32[4]{0:T(128)} %param.24) | copy-start | bytes 52
  59.6 16.6 %all-to-all-start.1 = ((bf16[8,288,128]{2,1,0:T(8,128)(2,1)}), bf16[8,288,128]{2,1,0:T(8,128)(2,1)S(1)}, u32[]{:S(2)}, u32[]{:S(2)}) async-start(bf16[8,288,128]{2,1,0:T(8,128)(2,1)} %pad_maximum_fusion.1), calls=%async_computation.1 | async-start | bytes 1179648 | tf_op jit(solution)/shard_map/all_to_all | solution.py:483
  76.1 7.2 %copy-start.9 = (bf16[8,288,128]{2,1,0:T(8,128)(2,1)}, bf16[8,288,128]{2,1,0:T(8,128)(2,1)S(1)}, u32[]{:S(2)}) copy-start(bf16[8,288,128]{2,1,0:T(8,128)(2,1)S(1)} %all-to-all-done.1.packs_ref) | copy-start | bytes 1769476
  76.9 16.8 %all-to-all-start.4 = ((bf16[16,1,128]{2,1,0:T(2,128)(2,1)}), bf16[16,1,128]{2,1,0:T(2,128)(2,1)S(1)}, u32[]{:S(2)}, u32[]{:S(2)}) async-start(bf16[16,1,128]{2,1,0:T(2,128)(2,1)} %all_to_all.47), calls=%async_computation.4 | async-start | bytes 16384 | tf_op jit(solution)/shard_map/all_to_all | solution.py:483
  93.7 35.6 %all-to-all-start.5 = ((bf16[16,256,256]{2,1,0:T(8,128)(2,1)}), bf16[16,256,256]{2,1,0:T(8,128)(2,1)S(1)}, u32[]{:S(2)}, u32[]{:S(2)}) async-start(bf16[16,256,256]{2,1,0:T(8,128)(2,1)} %bitcast.75), calls=%async_computation.5 | async-start | bytes 4194304 | tf_op jit(solution)/shard_map/all_to_all | solution.py:483
  129.4 36.0 %all-to-all-start.2 = ((bf16[16,256,256]{2,1,0:T(8,128)(2,1)}), bf16[16,256,256]{2,1,0:T(8,128)(2,1)}, u32[]{:S(2)}, u32[]{:S(2)}) async-start(bf16[16,256,256]{2,1,0:T(8,128)(2,1)} %bitcast.76), calls=%async_computation.2 | async-start | bytes 4194304 | tf_op jit(solution)/shard_map/all_to_all | solution.py:483
  143.5 1.0 copy-start
  165.4 24.0 %all-to-all-start.6 = ((bf16[16,32,1024]{2,1,0:T(8,128)(2,1)}), bf16[16,32,1024]{2,1,0:T(8,128)(2,1)S(1)}, u32[]{:S(2)}, u32[]{:S(2)}) async-start(bf16[16,32,1024]{2,1,0:T(8,128)(2,1)} %bitcast.61), calls=%async_computation.6 | async-start | bytes 2097152 | tf_op jit(solution)/shard_map/all_to_all | solution.py:483
  189.4 1.0 copy-start.7
  190.4 21.6 %all-to-all-start.3 = ((bf16[16,32,1024]{2,1,0:T(8,128)(2,1)}), bf16[16,32,1024]{2,1,0:T(8,128)(2,1)S(1)}, u32[]{:S(2)}, u32[]{:S(2)}) async-start(bf16[16,32,1024]{2,1,0:T(8,128)(2,1)} %bitcast.9), calls=%async_computation.3 | async-start | bytes 2097152 | tf_op jit(solution)/shard_map/all_to_all | solution.py:483
  194.9 29.8 %collective-permute-start.6 = (bf16[16,32,1024]{2,1,0:T(8,128)(2,1)}, bf16[16,32,1024]{2,1,0:T(8,128)(2,1)}, u32[]{:S(2)}, u32[]{:S(2)}) collective-permute-start(bf16[16,32,1024]{2,1,0:T(8,128)(2,1)} %copy-done.7), channel_id=1, source_target_pairs={{0,16},{16,32},{32,48},{48,0},{1,17},{17,33},{33,49},{49,1},{2,18}... | collective-permute-start | bytes 3145736 | tf_op jit(solution)/shard_map/ppermute | solution.py:487
  198.8 25.8 %collective-permute-start.8 = (bf16[16,32,1024]{2,1,0:T(8,128)(2,1)}, bf16[16,32,1024]{2,1,0:T(8,128)(2,1)}, u32[]{:S(2)}, u32[]{:S(2)}) collective-permute-start(bf16[16,32,1024]{2,1,0:T(8,128)(2,1)} %copy-done.7), channel_id=1, source_target_pairs={{0,48},{16,0},{32,16},{48,32},{1,49},{17,1},{33,17},{49,33},{2,50}... | collective-permute-start | bytes 3145736 | tf_op jit(solution)/shard_map/ppermute | solution.py:487
  212.1 23.9 %copy-start.1 = (bf16[16,32,1024]{2,1,0:T(8,128)(2,1)}, bf16[16,32,1024]{2,1,0:T(8,128)(2,1)S(1)}, u32[]{:S(2)}) copy-start(bf16[16,32,1024]{2,1,0:T(8,128)(2,1)S(1)} %all-to-all-done.3) | copy-start | bytes 3145732
  212.1 35.0 %collective-permute-start.12 = (bf16[16,32,1024]{2,1,0:T(8,128)(2,1)S(1)}, bf16[16,32,1024]{2,1,0:T(8,128)(2,1)S(1)}, u32[]{:S(2)}, u32[]{:S(2)}) collective-permute-start(bf16[16,32,1024]{2,1,0:T(8,128)(2,1)S(1)} %all-to-all-done.3), channel_id=1, source_target_pairs={{0,16},{16,32},{32,48},{48,0},{1,17},{17,33},{33,49},{49,1},{2,18}... | collective-permute-start | bytes 3145736 | tf_op jit(solution)/shard_map/ppermute | solution.py:487
  216.0 31.0 %collective-permute-start.13 = (bf16[16,32,1024]{2,1,0:T(8,128)(2,1)S(1)}, bf16[16,32,1024]{2,1,0:T(8,128)(2,1)}, u32[]{:S(2)}, u32[]{:S(2)}) collective-permute-start(bf16[16,32,1024]{2,1,0:T(8,128)(2,1)S(1)} %all-to-all-done.3), channel_id=1, source_target_pairs={{0,48},{16,0},{32,16},{48,32},{1,49},{17,1},{33,17},{49,33},{2,50}... | collective-permute-start | bytes 3145736 | tf_op jit(solution)/shard_map/ppermute | solution.py:487
  218.9 47.4 %collective-permute-start = (bf16[16,32,1024]{2,1,0:T(8,128)(2,1)S(1)}, bf16[16,32,1024]{2,1,0:T(8,128)(2,1)}, u32[]{:S(2)}, u32[]{:S(2)}) collective-permute-start(bf16[16,32,1024]{2,1,0:T(8,128)(2,1)S(1)} %all-to-all-done.3), channel_id=1, source_target_pairs={{0,64},{64,0},{1,65},{65,1},{2,66},{66,2},{3,67},{67,3},{4,68},{68... | collective-permute-start | bytes 3145736 | tf_op jit(solution)/shard_map/ppermute | solution.py:491
  224.7 44.5 %collective-permute-start.7 = (bf16[16,32,1024]{2,1,0:T(8,128)(2,1)}, bf16[16,32,1024]{2,1,0:T(8,128)(2,1)S(1)}, u32[]{:S(2)}, u32[]{:S(2)}) collective-permute-start(bf16[16,32,1024]{2,1,0:T(8,128)(2,1)} %collective-permute-done.6), channel_id=1, source_target_pairs={{0,64},{64,0},{1,65},{65,1},{2,66},{66,2},{3,67},{67,3},{4,68},{68... | collective-permute-start | bytes 3145736 | tf_op jit(solution)/shard_map/ppermute | solution.py:491
  224.7 62.7 %collective-permute-start.9 = (bf16[16,32,1024]{2,1,0:T(8,128)(2,1)}, bf16[16,32,1024]{2,1,0:T(8,128)(2,1)}, u32[]{:S(2)}, u32[]{:S(2)}) collective-permute-start(bf16[16,32,1024]{2,1,0:T(8,128)(2,1)} %collective-permute-done.8), channel_id=1, source_target_pairs={{0,64},{64,0},{1,65},{65,1},{2,66},{66,2},{3,67},{67,3},{4,68},{68... | collective-permute-start | bytes 3145736 | tf_op jit(solution)/shard_map/ppermute | solution.py:491
  247.0 5.5 %copy-start.3 = (bf16[16,32,1024]{2,1,0:T(8,128)(2,1)}, bf16[16,32,1024]{2,1,0:T(8,128)(2,1)S(1)}, u32[]{:S(2)}) copy-start(bf16[16,32,1024]{2,1,0:T(8,128)(2,1)S(1)} %collective-permute-done.12) | copy-start | bytes 3145732
  247.0 19.2 %collective-permute-start.16 = (bf16[8,32,1024]{2,1,0:T(8,128)(2,1)}, bf16[8,32,1024]{2,1,0:T(8,128)(2,1)}, u32[]{:S(2)}, u32[]{:S(2)}) collective-permute-start(bf16[8,32,1024]{2,1,0:T(8,128)(2,1)} %slice.92), channel_id=1, source_target_pairs={{0,16},{16,32},{32,48},{48,0},{1,17},{17,33},{33,49},{49,1},{2,18}... | collective-permute-start | bytes 1572872 | tf_op jit(solution)/shard_map/ppermute | solution.py:487
  247.0 19.5 %collective-permute-start.17 = (bf16[8,32,1024]{2,1,0:T(8,128)(2,1)}, bf16[8,32,1024]{2,1,0:T(8,128)(2,1)}, u32[]{:S(2)}, u32[]{:S(2)}) collective-permute-start(bf16[8,32,1024]{2,1,0:T(8,128)(2,1)} %slice.93), channel_id=1, source_target_pairs={{0,48},{16,0},{32,16},{48,32},{1,49},{17,1},{33,17},{49,33},{2,50}... | collective-permute-start | bytes 1572872 | tf_op jit(solution)/shard_map/ppermute | solution.py:487
  250.3 10.6 %copy-start.16 = (f32[4,1024]{1,0:T(4,128)S(1)}, f32[4,1024]{1,0:T(4,128)}, u32[]{:S(2)}) copy-start(f32[4,1024]{1,0:T(4,128)} %get-tuple-element.62) | copy-start | bytes 49156
  250.3 10.6 %copy-start.17 = (f32[4,1024]{1,0:T(4,128)S(1)}, f32[4,1024]{1,0:T(4,128)}, u32[]{:S(2)}) copy-start(f32[4,1024]{1,0:T(4,128)} %get-tuple-element.61) | copy-start | bytes 49156
  252.5 119.2 %all-to-all-start.7 = ((bf16[16,128,256]{2,1,0:T(8,128)(2,1)}), bf16[16,128,256]{2,1,0:T(8,128)(2,1)S(1)}, u32[]{:S(2)}, u32[]{:S(2)}) async-start(bf16[16,128,256]{2,1,0:T(8,128)(2,1)} %bitcast.45), calls=%async_computation.7 | async-start | bytes 2097152 | tf_op jit(solution)/shard_map/all_to_all | solution.py:483
  263.2 3.1 copy-start.8
  266.2 67.3 %collective-permute-start.5 = (bf16[16,32,1024]{2,1,0:T(8,128)(2,1)S(1)}, bf16[16,32,1024]{2,1,0:T(8,128)(2,1)S(1)}, u32[]{:S(2)}, u32[]{:S(2)}) collective-permute-start(bf16[16,32,1024]{2,1,0:T(8,128)(2,1)S(1)} %copy-done.8), channel_id=1, source_target_pairs={{0,64},{64,0},{1,65},{65,1},{2,66},{66,2},{3,67},{67,3},{4,68},{68... | collective-permute-start | bytes 3145736 | tf_op jit(solution)/shard_map/ppermute | solution.py:491
  266.3 42.2 %collective-permute-start.14 = (bf16[8,32,1024]{2,1,0:T(8,128)(2,1)S(1)}, bf16[8,32,1024]{2,1,0:T(8,128)(2,1)S(1)}, u32[]{:S(2)}, u32[]{:S(2)}) collective-permute-start(bf16[8,32,1024]{2,1,0:T(8,128)(2,1)S(1)} %slice.90), channel_id=1, source_target_pairs={{0,16},{16,32},{32,48},{48,0},{1,17},{17,33},{33,49},{49,1},{2,18}... | collective-permute-start | bytes 1572872 | tf_op jit(solution)/shard_map/ppermute | solution.py:487
  266.5 42.3 %collective-permute-start.15 = (bf16[8,32,1024]{2,1,0:T(8,128)(2,1)}, bf16[8,32,1024]{2,1,0:T(8,128)(2,1)S(1)}, u32[]{:S(2)}, u32[]{:S(2)}) collective-permute-start(bf16[8,32,1024]{2,1,0:T(8,128)(2,1)} %slice.91), channel_id=1, source_target_pairs={{0,48},{16,0},{32,16},{48,32},{1,49},{17,1},{33,17},{49,33},{2,50}... | collective-permute-start | bytes 1572872 | tf_op jit(solution)/shard_map/ppermute | solution.py:487
  269.2 36.5 %copy-start.2 = (bf16[16,32,1024]{2,1,0:T(8,128)(2,1)}, bf16[16,32,1024]{2,1,0:T(8,128)(2,1)S(1)}, u32[]{:S(2)}) copy-start(bf16[16,32,1024]{2,1,0:T(8,128)(2,1)S(1)} %collective-permute-done.7) | copy-start | bytes 3145732
  269.2 60.6 %collective-permute-start.1 = (bf16[16,32,1024]{2,1,0:T(8,128)(2,1)}, bf16[16,32,1024]{2,1,0:T(8,128)(2,1)S(1)}, u32[]{:S(2)}, u32[]{:S(2)}) collective-permute-start(bf16[16,32,1024]{2,1,0:T(8,128)(2,1)} %collective-permute-done), channel_id=1, source_target_pairs={{0,16},{16,32},{32,48},{48,0},{1,17},{17,33},{33,49},{49,1},{2,18}... | collective-permute-start | bytes 3145736 | tf_op jit(solution)/shard_map/ppermute | solution.py:487
  287.3 42.6 %collective-permute-start.2 = (bf16[16,32,1024]{2,1,0:T(8,128)(2,1)}, bf16[16,32,1024]{2,1,0:T(8,128)(2,1)S(1)}, u32[]{:S(2)}, u32[]{:S(2)}) collective-permute-start(bf16[16,32,1024]{2,1,0:T(8,128)(2,1)} %collective-permute-done), channel_id=1, source_target_pairs={{0,48},{16,0},{32,16},{48,32},{1,49},{17,1},{33,17},{49,33},{2,50}... | collective-permute-start | bytes 3145736 | tf_op jit(solution)/shard_map/ppermute | solution.py:487
  308.5 2.7 copy-start.11
  308.5 25.0 %collective-permute-start.10 = (bf16[8,32,1024]{2,1,0:T(8,128)(2,1)}, bf16[8,32,1024]{2,1,0:T(8,128)(2,1)S(1)}, u32[]{:S(2)}, u32[]{:S(2)}) collective-permute-start(bf16[8,32,1024]{2,1,0:T(8,128)(2,1)} %slice.88), channel_id=1, source_target_pairs={{0,16},{16,32},{32,48},{48,0},{1,17},{17,33},{33,49},{49,1},{2,18}... | collective-permute-start | bytes 1572872 | tf_op jit(solution)/shard_map/ppermute | solution.py:487
  308.8 2.4 copy-start.13
  308.8 24.8 %collective-permute-start.11 = (bf16[8,32,1024]{2,1,0:T(8,128)(2,1)}, bf16[8,32,1024]{2,1,0:T(8,128)(2,1)S(1)}, u32[]{:S(2)}, u32[]{:S(2)}) collective-permute-start(bf16[8,32,1024]{2,1,0:T(8,128)(2,1)} %slice.89), channel_id=1, source_target_pairs={{0,48},{16,0},{32,16},{48,32},{1,49},{17,1},{33,17},{49,33},{2,50}... | collective-permute-start | bytes 1572872 | tf_op jit(solution)/shard_map/ppermute | solution.py:487
  329.8 22.2 %copy-start.4 = (bf16[16,32,1024]{2,1,0:T(8,128)(2,1)}, bf16[16,32,1024]{2,1,0:T(8,128)(2,1)S(1)}, u32[]{:S(2)}) copy-start(bf16[16,32,1024]{2,1,0:T(8,128)(2,1)S(1)} %collective-permute-done.1) | copy-start | bytes 3145732
  329.9 22.2 %collective-permute-start.3 = (bf16[8,32,1024]{2,1,0:T(8,128)(2,1)S(1)}, bf16[8,32,1024]{2,1,0:T(8,128)(2,1)S(1)}, u32[]{:S(2)}, u32[]{:S(2)}) collective-permute-start(bf16[8,32,1024]{2,1,0:T(8,128)(2,1)S(1)} %slice.85), channel_id=1, source_target_pairs={{0,16},{16,32},{32,48},{48,0},{1,17},{17,33},{33,49},{49,1},{2,18}... | collective-permute-start | bytes 1572872 | tf_op jit(solution)/shard_map/ppermute | solution.py:487
  330.0 22.1 %copy-start.5 = (bf16[16,32,1024]{2,1,0:T(8,128)(2,1)}, bf16[16,32,1024]{2,1,0:T(8,128)(2,1)S(1)}, u32[]{:S(2)}) copy-start(bf16[16,32,1024]{2,1,0:T(8,128)(2,1)S(1)} %collective-permute-done.2) | copy-start | bytes 3145732
  331.0 21.1 %collective-permute-start.4 = (bf16[8,32,1024]{2,1,0:T(8,128)(2,1)}, bf16[8,32,1024]{2,1,0:T(8,128)(2,1)S(1)}, u32[]{:S(2)}, u32[]{:S(2)}) collective-permute-start(bf16[8,32,1024]{2,1,0:T(8,128)(2,1)} %slice.86), channel_id=1, source_target_pairs={{0,48},{16,0},{32,16},{48,32},{1,49},{17,1},{33,17},{49,33},{2,50}... | collective-permute-start | bytes 1572872 | tf_op jit(solution)/shard_map/ppermute | solution.py:487
  333.5 1.0 copy-start.6
  333.5 1.2 copy-start.10
  333.6 1.3 copy-start.12
  352.1 0.8 copy-start.14
  352.1 0.9 copy-start.15
  372.6 19.0 %all-to-all-start.8 = ((f32[128,1,16]{2,1,0:T(1,128)}), f32[128,1,16]{2,1,0:T(1,128)S(1)}, u32[]{:S(2)}, u32[]{:S(2)}) async-start(f32[128,1,16]{2,1,0:T(1,128)} %bitcast.46), calls=%async_computation.8 | async-start | bytes 131072 | tf_op jit(solution)/shard_map/all_to_all | solution.py:483
Sparse Core Ops, SparseCore 0:
  40.8 73.6 all-gather.1

commit v2 on v1

--- a/solution.py
+++ b/solution.py
@@ -54,38 +54,32 @@
     for c in range(spans):
         cumc_ref[c] = turned[:, 8 * c : 8 * c + 8]
 
-    def forward(c, carry):
-        state, run = carry
+    def spans_both(i, carry):
+        state, run, after, later = carry
+        c, d = i, spans - 1 - i
         sl_ref[c] = state.astype(BF)
+        gl_ref[d] = after.astype(BF)
         dpre_ref[c] = jnp.exp(-run)
+        dpost_ref[d] = jnp.exp(-later)
         at = pl.ds(pl.multiple_of(c * L, L), L)
+        to = pl.ds(pl.multiple_of(d * L, L), L)
         cols = cumc_ref[c]
         last = jnp.broadcast_to(cumr_ref[c][:, L - 1 : L], (8, NST))
+        final = jnp.broadcast_to(cumr_ref[d][:, L - 1 : L], (8, NST))
         tail = jnp.exp(jnp.minimum(cols - cols[L - 1 : L, :], 0.0))
-        decayed = (x_ref[at, :].astype(F32) * over_heads(tail)).astype(BF)
-        fresh = dot(decayed, b_ref[at, :], TN)
-        return (head_rows(jnp.exp(-last)) * state + fresh, run + last)
+        x_part = (x_ref[at, :].astype(F32) * over_heads(tail)).astype(BF)
+        g_part = (g_ref[to, :].astype(F32) * over_heads(jnp.exp(-cumc_ref[d]))).astype(BF)
+        state = head_rows(jnp.exp(-last)) * state + dot(x_part, b_ref[at, :], TN)
+        after = head_rows(jnp.exp(-final)) * after + dot(g_part, c_ref[to, :], TN)
+        return (state, run + last, after, later + final)
 
     zero = (jnp.zeros((HP, NST), F32), jnp.zeros((8, NST), F32))
-    state, run = lax.fori_loop(0, spans, forward, zero)
+    state, run, after, _ = lax.fori_loop(0, spans, spans_both, zero + zero)
     pack_ref[0:HP, :] = state.astype(BF)
+    pack_ref[HP : 2 * HP, :] = after.astype(BF)
     total = jnp.exp(-run)
     high = total.astype(BF).astype(F32)
     pack_ref[2 * HP : 2 * HP + 16, :] = jnp.concatenate([high, total - high], axis=0).astype(BF)
-
-    def backward(i, carry):
-        state, run = carry
-        c = spans - 1 - i
-        gl_ref[c] = state.astype(BF)
-        dpost_ref[c] = jnp.exp(-run)
-        at = pl.ds(pl.multiple_of(c * L, L), L)
-        last = jnp.broadcast_to(cumr_ref[c][:, L - 1 : L], (8, NST))
-        decayed = (g_ref[at, :].astype(F32) * over_heads(jnp.exp(-cumc_ref[c]))).astype(BF)
-        fresh = dot(decayed, c_ref[at, :], TN)
-        return (head_rows(jnp.exp(-last)) * state + fresh, run + last)
-
-    state, run = lax.fori_loop(0, spans, backward, zero)
-    pack_ref[HP : 2 * HP, :] = state.astype(BF)
 
 
 def local_states(x, g, b, c, step, alog):
@@ -347,64 +341,51 @@
 
 
 def expert_kernel(half, at_ref, own, left, right, low, high, w_hbm, saved, gates, *rest):
-    out, route_ref, xbuf, wbuf, sbuf, gbuf, obuf, up_ref, psum_ref, mixed_ref, grad_ref, sems = rest[
-        -12:
-    ]
+    out, route_ref, xbuf, wbuf, sbuf, gbuf, obuf, up_ref, psum_ref, mixed_ref, grad_ref, sems, x_sems = (
+        rest[-13:]
+    )
     x_at, y_at = at_ref[0], at_ref[1]
     saved_copy = pltpu.make_async_copy(saved.at[y_at, :, half], sbuf.reshape(4, 128, 2, 896), sems.at[4])
     gates_copy = pltpu.make_async_copy(gates.at[y_at, :, half], gbuf.reshape(4, 128, 1), sems.at[5])
-    weights = [
-        pltpu.make_async_copy(
-            w_hbm.at[256 * i : min(256 * (i + 1), 896), :],
-            wbuf.at[256 * i : min(256 * (i + 1), 896), :],
-            sems.at[i],
-        )
-        for i in range(4)
-    ]
-    copies = []
-    for piece, step, first in ((own, 0, 0), (left, 3, 0), (right, 1, 0), (low, 2, 0), (high, 2, 2)):
-        source = lax.rem(x_at + step, 4)
-        for q in range(piece.shape[0]):
+    lanes_of = lambda q: pl.ds(pl.multiple_of(q * 1024, 1024), 1024)
+    weights_of = lambda q: pltpu.make_async_copy(
+        w_hbm.at[:, lanes_of(q)], wbuf.at[:, lanes_of(q)], sems.at[q]
+    )
+    sources = [lax.rem(x_at + step, 4) for step in (0, 3, 1, 2)]
+    for q in range(4):
+        far = (low, q) if q < 2 else (high, q - 2)
+        for j, (piece, at) in enumerate(((own, q), (left, q), (right, q), far)):
             for k in range(2):
-                copies.append(
-                    pltpu.make_async_copy(
-                        piece.at[q, :, k],
-                        xbuf.at[first + q, source, k],
-                        sems.at[6 + len(copies)],
-                    )
-                )
-    weights[0].start()
-    for copy in copies:
-        copy.start()
-    for copy in weights[1:]:
-        copy.start()
+                pltpu.make_async_copy(
+                    piece.at[at, :, k], xbuf.at[q, sources[j], k], x_sems.at[q, j, k]
+                ).start()
+        weights_of(q).start()
     gates_copy.start()
     saved_copy.start()
-    for copy in copies:
-        copy.wait()
-
-    def tile(at, width):
-        here = pl.ds(at, width)
-        up_ref[:, here] = jnp.zeros((512, width), F32)
-
-        def step(q, carry):
+    up_ref[...] = jnp.zeros_like(up_ref)
+
+    def by_quarter(q, carry):
+        for j in range(4):
+            for k in range(2):
+                pltpu.make_async_copy(
+                    own.at[q, :, k], xbuf.at[q, sources[j], k], x_sems.at[q, j, k]
+                ).wait()
+        weights_of(q).wait()
+
+        def tile(at, width):
+            here = pl.ds(at, width)
             piece = xbuf[q].reshape(512, 1024)
-            lanes = pl.ds(pl.multiple_of(q * 1024, 1024), 1024)
-            up_ref[:, here] += dot(piece, wbuf[here, lanes], NT)
+            up_ref[:, here] += dot(piece, wbuf[here, lanes_of(q)], NT)
+
+        def wide(i, carry):
+            tile(pl.multiple_of(i * 256, 256), 256)
             return carry
 
-        lax.fori_loop(0, 4, step, 0)
-
-    def later(i, carry):
-        tile(pl.multiple_of(i * 256, 256), 256)
+        lax.fori_loop(0, 3, wide, 0)
+        tile(768, 128)
         return carry
 
-    weights[0].wait()
-    tile(0, 256)
-    for copy in (weights[1], weights[2], weights[3]):
-        copy.wait()
-    lax.fori_loop(1, 3, later, 0)
-    tile(768, 128)
+    lax.fori_loop(0, 4, by_quarter, 0)
     gates_copy.wait()
     saved_copy.wait()
     count = 32
@@ -431,12 +412,20 @@
         psum_ref[rows, :] = routed
         return carry
 
-    lax.fori_loop(0, 512 // count, group, 0)
-    out_copy = pltpu.make_async_copy(obuf.reshape(4, 128, 2, 896), out.at[y_at, :, half], sems.at[4])
-    out_copy.start()
+    def out_of(j):
+        rows = pl.ds(pl.multiple_of(j * 128, 128), 128)
+        return pltpu.make_async_copy(obuf.at[rows], out.at[y_at, j, half], sems.at[6 + j])
+
+    def block(j, carry):
+        lax.fori_loop(j * (128 // count), (j + 1) * (128 // count), group, 0)
+        out_of(j).start()
+        return carry
+
+    lax.fori_loop(0, 4, block, 0)
     ones = jnp.ones((8, 128), F32)
     route_ref[...] = dot(ones, psum_ref[...], NT, precision=lax.Precision.HIGHEST)
-    out_copy.wait()
+    for j in range(4):
+        out_of(j).wait()
 
 
 def expert_grads(half, at, pieces, weight, saved, gates, before):
@@ -463,7 +452,8 @@
             pltpu.VMEM((512, 128), F32),
             pltpu.VMEM((64, 128), F32),
             pltpu.VMEM((64, 128), F32),
-            pltpu.SemaphoreType.DMA((40,)),
+            pltpu.SemaphoreType.DMA((12,)),
+            pltpu.SemaphoreType.DMA((4, 4, 2)),
         ],
         input_output_aliases={} if before is None else {9: 0},
         compiler_params=pltpu.CompilerParams(vmem_limit_bytes=56 << 20),

time: 402 us -> 396 us (0.985)
  Pallas kernels: 133 us -> 126 us
    pallas_call x1, Pallas kernels: 15.6 us -> 11.1 us  [local_states(): pl.pallas_call(states_kernel, out_shape=out, scratch_shapes=[pltpu.VMEM((...]
  transfers between devices with their start and end apart: 27 -> 27, of which waited for: 9 -> 9; matrix products, arithmetic and copies ran while one was open for 6% -> 6% of each run, Pallas kernels for 32% -> 31%
where the time goes in v2:
time: 396 us; the launch traced here: 393 us
  Pallas kernels  126 us (32%)
  waiting for transfers between devices  111 us (28%)
  starting transfers between devices  81.3 us (21%)
  blocking collectives  28.6 us (7%)
  local copies, waits for them, and re-layouts  26.1 us (7%)
  between operations  14.4 us (4%)
  other arithmetic  5.87 us (1%)
    all_to_all x8, waiting for transfers between devices, a2a(): return lax.all_to_all(array, axis, split_axis=0, concat_axis=0, tiled=True)  80.4 us
    pallas_call x4, Pallas kernels, expert_grads(): pl.pallas_call(functools.partial(expert_kernel, half), in_specs=[pl.Block...  66.3 us
    all_to_all x8, starting transfers between devices, a2a(): return lax.all_to_all(array, axis, split_axis=0, concat_axis=0, tiled=True)  54.3 us
    all_to_all x1, blocking collectives, a2a(): return lax.all_to_all(array, axis, split_axis=0, concat_axis=0, tiled=True)  28.6 us
    ppermute x14, starting transfers between devices, shifted(): return lax.ppermute(array, 'x', [(i, (i + by) % 4) for i in range(4)])  24.6 us
    pallas_call x2, Pallas kernels, span_grads(): pl.pallas_call(grads_kernel, grid=(spans,), in_specs=[pl.BlockSpec(memory...  20.7 us
    ppermute x4, waiting for transfers between devices, other_row(): return lax.ppermute(array, 'yl', [(0, 1), (1, 0)])  18 us
    pallas_call x2, Pallas kernels, expert_rows(): pl.pallas_call(rows_kernel, grid=(4,), in_specs=[pl.BlockSpec((16, 256, 2...  14.4 us
  transfers between devices with their start and end apart: 27, of which 9 were waited for; matrix products, arithmetic and copies ran while one was open for 6% of the time, Pallas kernels for 31%

profile of v2, /device:TPU:1, one launch (start us, length us, event | category | flops | bytes accessed | tf_op | source)
XLA Modules:
  0.0 393.1 jit_solution(11155879073041429139)
XLA Ops:
  7.2 1.6 routing.1
  8.8 2.6 first_exchange.1
  11.4 28.6 %all_to_all.57.res_ref = bf16[4,176,1024]{2,1,0:T(8,128)(2,1)S(1)} all-to-all(bf16[4,176,1024]{2,1,0:T(8,128)(2,1)} %first_exchange.1), channel_id=1, replica_groups=mesh['yl'=2,'x'=4,'yh'=2,'zh'=2,'zl'=2,'core'=2] {'yh','zh'}, dimensions={0} | all-to-all | bytes 2883584 | tf_op jit(solution)/shard_map/all_to_all | solution.py:473
  41.4 11.1 %states.1 = (f32[16,8,128]{2,1,0:T(8,128)}, f32[16,128,8]{2,1,0:T(8,128)}, bf16[16,256,128]{2,1,0:T(8,128)(2,1)}, bf16[16,256,128]{2,1,0:T(8,128)(2,1)}, f32[16,...) custom-call(bf16[2048,256]{1,0:T(8,128)(2,1)} %x_ref.5, bf16[2048,256]{1,0:T(8,128)(2,1)} %g_ref.5, ...), custom_call_target="tpu_custom_call" | custom-call | flops 8000000000 | bytes 1048576 | tf_op jit(solution)/shard_map/states/pallas_call | solution.py:96
  55.1 4.1 %all-to-all-start.1 = ((bf16[8,288,128]{2,1,0:T(8,128)(2,1)}), bf16[8,288,128]{2,1,0:T(8,128)(2,1)S(1)}, u32[]{:S(2)}, u32[]{:S(2)}) async-start(bf16[8,288,128]{2,1,0:T(8,128)(2,1)} %pad_maximum_fusion.1), calls=%async_computation.1 | async-start | bytes 1179648 | tf_op jit(solution)/shard_map/all_to_all | solution.py:473
  59.9 10.5 %all-to-all-done.1.packs_ref = bf16[8,288,128]{2,1,0:T(8,128)(2,1)S(1)} async-done(((bf16[8,288,128]{2,1,0:T(8,128)(2,1)}), bf16[8,288,128]{2,1,0:T(8,128)(2,1)S(1)}, u32[]{:S(2)}, u32[]{:S(2)}) %all-to-all-start.1) | async-done | bytes 589856 | tf_op jit(solution)/shard_map/all_to_all | solution.py:473
  71.2 7.7 %all-to-all-start.4 = ((bf16[16,1,128]{2,1,0:T(2,128)(2,1)}), bf16[16,1,128]{2,1,0:T(2,128)(2,1)S(1)}, u32[]{:S(2)}, u32[]{:S(2)}) async-start(bf16[16,1,128]{2,1,0:T(2,128)(2,1)} %all_to_all.47), calls=%async_computation.4 | async-start | bytes 16384 | tf_op jit(solution)/shard_map/all_to_all | solution.py:473
  78.9 10.4 %span_grads.3 = (bf16[4,4,2,128,256]{4,3,2,1,0:T(8,128)(2,1)}, bf16[1024,256]{1,0:T(8,128)(2,1)}, f32[4,1024]{1,0:T(4,128)}) custom-call(s32[1]{0:T(128)} %bitcast.2.me_ref, bf16[2048,256]{1,0:T(8,128)(2,1)} %x_ref.5, bf16[2048,256]{1,0:T(8,128)(2,1)} %g_ref.5, bf16[2048,128]{1,0:T(8,128)(2,1)} %b_ref.5, bf16[2048,128]{1,0:T(8,128)(2,1)} %c_ref.5, ...), custom_call_target="tpu_custom_call" | custom-call | flops 5000000000 | bytes 1048576 | tf_op jit(solution)/shard_map/span_grads/pallas_call | solution.py:202
  89.3 7.2 %all-to-all-start.5 = ((bf16[16,256,256]{2,1,0:T(8,128)(2,1)}), bf16[16,256,256]{2,1,0:T(8,128)(2,1)S(1)}, u32[]{:S(2)}, u32[]{:S(2)}) async-start(bf16[16,256,256]{2,1,0:T(8,128)(2,1)} %bitcast.75), calls=%async_computation.5 | async-start | bytes 4194304 | tf_op jit(solution)/shard_map/all_to_all | solution.py:473
  96.5 10.3 %span_grads.2 = (bf16[4,4,2,128,256]{4,3,2,1,0:T(8,128)(2,1)}, bf16[1024,256]{1,0:T(8,128)(2,1)}, f32[4,1024]{1,0:T(4,128)}) custom-call(s32[1]{0:T(128)} %bitcast.2.me_ref, bf16[2048,256]{1,0:T(8,128)(2,1)} %x_ref.5, bf16[2048,256]{1,0:T(8,128)(2,1)} %g_ref.5, bf16[2048,128]{1,0:T(8,128)(2,1)} %b_ref.5, bf16[2048,128]{1,0:T(8,128)(2,1)} %c_ref.5, ...), custom_call_target="tpu_custom_call" | custom-call | flops 5000000000 | bytes 1048576 | tf_op jit(solution)/shard_map/span_grads/pallas_call | solution.py:202
  106.8 20.0 %all-to-all-done.5.x_ref = bf16[16,256,256]{2,1,0:T(8,128)(2,1)S(1)} async-done(((bf16[16,256,256]{2,1,0:T(8,128)(2,1)}), bf16[16,256,256]{2,1,0:T(8,128)(2,1)S(1)}, u32[]{:S(2)}, u32[]{:S(2)}) %all-to-all-start.5) | async-done | bytes 2097184 | tf_op jit(solution)/shard_map/all_to_all | solution.py:473
  126.8 6.4 %all-to-all-start.2 = ((bf16[16,256,256]{2,1,0:T(8,128)(2,1)}), bf16[16,256,256]{2,1,0:T(8,128)(2,1)}, u32[]{:S(2)}, u32[]{:S(2)}) async-start(bf16[16,256,256]{2,1,0:T(8,128)(2,1)} %bitcast.76), calls=%async_computation.2 | async-start | bytes 4194304 | tf_op jit(solution)/shard_map/all_to_all | solution.py:473
  133.2 6.5 %expert_rows.3 = bf16[16,2,16,1024]{3,2,1,0:T(8,128)(2,1)S(1)} custom-call(bf16[16,256,256]{2,1,0:T(8,128)(2,1)S(1)} %all-to-all-done.5.x_ref, bf16[8,4,4,32,1024]{4,3,2,1,0:T(8,128)(2,1)} %bitcast.67, bf16[4,176,1024]{2,1,0:T(8,128)(2,1)S(1)} %all_to_all.57.res_ref), custom_call_target="tpu_custom_call" | custom-call | flops 3000000000 | bytes 1048576 | tf_op jit(solution)/shard_map/expert_rows/pallas_call | solution.py:304
  140.7 21.0 %all-to-all-done.2.x_ref = bf16[16,256,256]{2,1,0:T(8,128)(2,1)} async-done(((bf16[16,256,256]{2,1,0:T(8,128)(2,1)}), bf16[16,256,256]{2,1,0:T(8,128)(2,1)}, u32[]{:S(2)}, u32[]{:S(2)}) %all-to-all-start.2) | async-done | bytes 2097184 | tf_op jit(solution)/shard_map/all_to_all | solution.py:473
  161.6 6.9 %all-to-all-start.6 = ((bf16[16,32,1024]{2,1,0:T(8,128)(2,1)}), bf16[16,32,1024]{2,1,0:T(8,128)(2,1)S(1)}, u32[]{:S(2)}, u32[]{:S(2)}) async-start(bf16[16,32,1024]{2,1,0:T(8,128)(2,1)} %bitcast.61), calls=%async_computation.6 | async-start | bytes 2097152 | tf_op jit(solution)/shard_map/all_to_all | solution.py:473
  168.6 7.9 %expert_rows.2 = bf16[16,2,16,1024]{3,2,1,0:T(8,128)(2,1)} custom-call(bf16[16,256,256]{2,1,0:T(8,128)(2,1)} %all-to-all-done.2.x_ref, bf16[8,4,4,32,1024]{4,3,2,1,0:T(8,128)(2,1)} %bitcast.68, bf16[4,176,1024]{2,1,0:T(8,128)(2,1)S(1)} %all_to_all.57.res_ref), custom_call_target="tpu_custom_call" | custom-call | flops 3000000000 | bytes 1048576 | tf_op jit(solution)/shard_map/expert_rows/pallas_call | solution.py:304
  176.5 9.2 %all-to-all-done.6 = bf16[16,32,1024]{2,1,0:T(8,128)(2,1)S(1)} async-done(((bf16[16,32,1024]{2,1,0:T(8,128)(2,1)}), bf16[16,32,1024]{2,1,0:T(8,128)(2,1)S(1)}, u32[]{:S(2)}, u32[]{:S(2)}) %all-to-all-start.6) | async-done | bytes 1048608 | tf_op jit(solution)/shard_map/all_to_all | solution.py:473
  186.7 4.5 %all-to-all-start.3 = ((bf16[16,32,1024]{2,1,0:T(8,128)(2,1)}), bf16[16,32,1024]{2,1,0:T(8,128)(2,1)S(1)}, u32[]{:S(2)}, u32[]{:S(2)}) async-start(bf16[16,32,1024]{2,1,0:T(8,128)(2,1)} %bitcast.9), calls=%async_computation.3 | async-start | bytes 2097152 | tf_op jit(solution)/shard_map/all_to_all | solution.py:473
  191.1 3.2 collective-permute-start.6
  194.3 3.2 collective-permute-start.8
  197.6 10.7 %all-to-all-done.3 = bf16[16,32,1024]{2,1,0:T(8,128)(2,1)S(1)} async-done(((bf16[16,32,1024]{2,1,0:T(8,128)(2,1)}), bf16[16,32,1024]{2,1,0:T(8,128)(2,1)S(1)}, u32[]{:S(2)}, u32[]{:S(2)}) %all-to-all-start.3) | async-done | bytes 1048608 | tf_op jit(solution)/shard_map/all_to_all | solution.py:473
  208.3 3.2 collective-permute-start.12
  211.5 3.1 collective-permute-start.13
  215.7 5.4 %collective-permute-done.6 = bf16[16,32,1024]{2,1,0:T(8,128)(2,1)} collective-permute-done((bf16[16,32,1024]{2,1,0:T(8,128)(2,1)}, bf16[16,32,1024]{2,1,0:T(8,128)(2,1)}, u32[]{:S(2)}, u32[]{:S(2)}) %collective-permute-start.6) | collective-permute-done | bytes 1048608 | tf_op jit(solution)/shard_map/ppermute | solution.py:477
  221.4 1.1 collective-permute-start.9
  223.3 9.1 %turned.1.w_hbm = bf16[896,4096]{1,0:T(8,128)(2,1)} custom-call(bf16[896,4096]{1,0:T(8,128)(2,1)} %bitcast.69), custom_call_target="tpu_custom_call" | custom-call | flops 3000000000 | bytes 1048576 | tf_op jit(solution)/shard_map/turned/pallas_call | solution.py:332
  232.4 1.9 slice.92
  234.2 1.9 slice.93
  236.1 7.3 %collective-permute-done.12 = bf16[16,32,1024]{2,1,0:T(8,128)(2,1)S(1)} collective-permute-done((bf16[16,32,1024]{2,1,0:T(8,128)(2,1)S(1)}, bf16[16,32,1024]{2,1,0:T(8,128)(2,1)S(1)}, u32[]{:S(2)}, u32[]{:S(2)}) %collective-permute-start.12) | collective-permute-done | bytes 1048608 | tf_op jit(solution)/shard_map/ppermute | solution.py:477
  243.4 2.7 collective-permute-start.17
  246.7 2.3 pad_maximum_fusion
  248.9 8.3 %all-to-all-start.7 = ((bf16[16,128,256]{2,1,0:T(8,128)(2,1)}), bf16[16,128,256]{2,1,0:T(8,128)(2,1)S(1)}, u32[]{:S(2)}, u32[]{:S(2)}) async-start(bf16[16,128,256]{2,1,0:T(8,128)(2,1)} %bitcast.45), calls=%async_computation.7 | async-start | bytes 2097152 | tf_op jit(solution)/shard_map/all_to_all | solution.py:473
  258.0 1.6 reshape.170.gates
  259.6 1.2 slice.90
  260.7 1.9 slice.91
  263.0 2.7 collective-permute-start.15
  265.7 18.0 %collective-permute-done.9 = bf16[16,32,1024]{2,1,0:T(8,128)(2,1)} collective-permute-done((bf16[16,32,1024]{2,1,0:T(8,128)(2,1)}, bf16[16,32,1024]{2,1,0:T(8,128)(2,1)}, u32[]{:S(2)}, u32[]{:S(2)}) %collective-permute-start.9) | collective-permute-done | bytes 1048608 | tf_op jit(solution)/shard_map/ppermute | solution.py:481
  283.7 1.2 collective-permute-start.2
  284.9 16.6 %expert_grads.4 = (bf16[2,4,2,128,2,896]{5,4,3,2,1,0:T(2,128)(2,1)}, f32[8,512]{1,0:T(8,128)}) custom-call(s32[2]{0:T(128)} %pad_add_fusion.1.at_ref, bf16[4,4,2,16,1024]{4,3,2,1,0:T(8,128)(2,1)} %bitcast.78, bf16[4,4,2,16,1024]{4,3,2,1,0:T(8,128)(2,1)} %bitcast.33.left, bf16[4,4,2,16,1024]{4,3,2,1,0:T(8,128)(2,1)} %bitcast.34.right, ...), custom_call_target="tpu_custom_call" | custom-call | flops 6000000000 | bytes 1048576 | tf_op jit(solution)/shard_map/expert_grads/pallas_call | solution.py:437
  302.4 1.9 slice.89
  304.5 2.4 collective-permute-start.11
  306.9 16.6 %expert_grads.5 = (bf16[2,4,2,128,2,896]{5,4,3,2,1,0:T(2,128)(2,1)}, f32[8,512]{1,0:T(8,128)}) custom-call(s32[2]{0:T(128)} %pad_add_fusion.1.at_ref, bf16[4,4,2,16,1024]{4,3,2,1,0:T(8,128)(2,1)} %bitcast.70, bf16[4,4,2,16,1024]{4,3,2,1,0:T(8,128)(2,1)} %bitcast.72, bf16[4,4,2,16,1024]{4,3,2,1,0:T(8,128)(2,1)} %bitcast.29.right, ...), custom_call_target="tpu_custom_call", output_to_operand_aliasing={{0}: (9, {})} | custom-call | flops 6000000000 | bytes 1048576 | tf_op jit(solution)/shard_map/expert_grads/pallas_call | solution.py:437
  325.1 1.0 slice.86
  326.1 2.5 collective-permute-start.4
  330.0 16.6 %expert_grads.6 = (bf16[2,4,2,128,2,896]{5,4,3,2,1,0:T(2,128)(2,1)}, f32[8,512]{1,0:T(8,128)}) custom-call(s32[2]{0:T(128)} %pad_add_fusion.at_ref, bf16[4,4,2,16,1024]{4,3,2,1,0:T(8,128)(2,1)} %bitcast.77, bf16[4,4,2,16,1024]{4,3,2,1,0:T(8,128)(2,1)} %bitcast.71, bf16[4,4,2,16,1024]{4,3,2,1,0:T(8,128)(2,1)} %bitcast.23.right, ...), custom_call_target="tpu_custom_call", output_to_operand_aliasing={{0}: (9, {})} | custom-call | flops 6000000000 | bytes 1048576 | tf_op jit(solution)/shard_map/expert_grads/pallas_call | solution.py:437
  347.6 16.6 %expert_grads.7 = (bf16[2,4,2,128,2,896]{5,4,3,2,1,0:T(2,128)(2,1)}, f32[8,512]{1,0:T(8,128)}) custom-call(s32[2]{0:T(128)} %pad_add_fusion.at_ref, bf16[4,4,2,16,1024]{4,3,2,1,0:T(8,128)(2,1)} %bitcast.10.own, bf16[4,4,2,16,1024]{4,3,2,1,0:T(8,128)(2,1)} %bitcast.73, bf16[4,4,2,16,1024]{4,3,2,1,0:T(8,128)(2,1)} %bitcast.74, ...), custom_call_target="tpu_custom_call", output_to_operand_aliasing={{0}: (9, {})} | custom-call | flops 6000000000 | bytes 1048576 | tf_op jit(solution)/shard_map/expert_grads/pallas_call | solution.py:437
  366.5 9.2 %all-to-all-start.8 = ((f32[128,1,16]{2,1,0:T(1,128)}), f32[128,1,16]{2,1,0:T(1,128)S(1)}, u32[]{:S(2)}, u32[]{:S(2)}) async-start(f32[128,1,16]{2,1,0:T(1,128)} %bitcast.46), calls=%async_computation.8 | async-start | bytes 131072 | tf_op jit(solution)/shard_map/all_to_all | solution.py:473
  376.4 9.1 %all-to-all-done.8 = f32[128,1,16]{2,1,0:T(1,128)S(1)} async-done(((f32[128,1,16]{2,1,0:T(1,128)}), f32[128,1,16]{2,1,0:T(1,128)S(1)}, u32[]{:S(2)}, u32[]{:S(2)}) %all-to-all-start.8) | async-done | bytes 8224 | tf_op jit(solution)/shard_map/all_to_all | solution.py:473
  (106 shorter events, 20.1 us)
Async XLA Ops:
  7.2 126.0 %all-gather.2.cloned.1.call-start = ((), (), s32[]{:S(2)}) async-start(), calls=%async_computation.9 | async-start | bytes 8650752 | tf_op jit(solution)/shard_map/all_gather | solution.py:502
  11.4 29.4 %copy-start.19 = (f32[4]{0:T(128)S(1)}, f32[4]{0:T(128)}, u32[]{:S(2)}) copy-start(f32[4]{0:T(128)} %param.23) | copy-start | bytes 52
  41.4 11.8 %copy-start.18 = (bf16[16,16]{1,0:T(8,128)(2,1)S(1)}, bf16[16,16]{1,0:T(8,128)(2,1)}, u32[]{:S(2)}) copy-start(bf16[16,16]{1,0:T(8,128)(2,1)} %get-tuple-element.43) | copy-start | bytes 1540
  52.5 6.7 %copy-start.20 = (f32[4]{0:T(128)S(1)}, f32[4]{0:T(128)}, u32[]{:S(2)}) copy-start(f32[4]{0:T(128)} %param.24) | copy-start | bytes 52
  55.1 15.3 %all-to-all-start.1 = ((bf16[8,288,128]{2,1,0:T(8,128)(2,1)}), bf16[8,288,128]{2,1,0:T(8,128)(2,1)S(1)}, u32[]{:S(2)}, u32[]{:S(2)}) async-start(bf16[8,288,128]{2,1,0:T(8,128)(2,1)} %pad_maximum_fusion.1), calls=%async_computation.1 | async-start | bytes 1179648 | tf_op jit(solution)/shard_map/all_to_all | solution.py:473
  70.4 8.5 %copy-start.9 = (bf16[8,288,128]{2,1,0:T(8,128)(2,1)}, bf16[8,288,128]{2,1,0:T(8,128)(2,1)S(1)}, u32[]{:S(2)}) copy-start(bf16[8,288,128]{2,1,0:T(8,128)(2,1)S(1)} %all-to-all-done.1.packs_ref) | copy-start | bytes 1769476
  71.2 18.1 %all-to-all-start.4 = ((bf16[16,1,128]{2,1,0:T(2,128)(2,1)}), bf16[16,1,128]{2,1,0:T(2,128)(2,1)S(1)}, u32[]{:S(2)}, u32[]{:S(2)}) async-start(bf16[16,1,128]{2,1,0:T(2,128)(2,1)} %all_to_all.47), calls=%async_computation.4 | async-start | bytes 16384 | tf_op jit(solution)/shard_map/all_to_all | solution.py:473
  89.3 37.5 %all-to-all-start.5 = ((bf16[16,256,256]{2,1,0:T(8,128)(2,1)}), bf16[16,256,256]{2,1,0:T(8,128)(2,1)S(1)}, u32[]{:S(2)}, u32[]{:S(2)}) async-start(bf16[16,256,256]{2,1,0:T(8,128)(2,1)} %bitcast.75), calls=%async_computation.5 | async-start | bytes 4194304 | tf_op jit(solution)/shard_map/all_to_all | solution.py:473
  126.8 34.8 %all-to-all-start.2 = ((bf16[16,256,256]{2,1,0:T(8,128)(2,1)}), bf16[16,256,256]{2,1,0:T(8,128)(2,1)}, u32[]{:S(2)}, u32[]{:S(2)}) async-start(bf16[16,256,256]{2,1,0:T(8,128)(2,1)} %bitcast.76), calls=%async_computation.2 | async-start | bytes 4194304 | tf_op jit(solution)/shard_map/all_to_all | solution.py:473
  139.7 1.0 copy-start
  161.6 24.0 %all-to-all-start.6 = ((bf16[16,32,1024]{2,1,0:T(8,128)(2,1)}), bf16[16,32,1024]{2,1,0:T(8,128)(2,1)S(1)}, u32[]{:S(2)}, u32[]{:S(2)}) async-start(bf16[16,32,1024]{2,1,0:T(8,128)(2,1)} %bitcast.61), calls=%async_computation.6 | async-start | bytes 2097152 | tf_op jit(solution)/shard_map/all_to_all | solution.py:473
  185.7 1.0 copy-start.7
  186.7 21.6 %all-to-all-start.3 = ((bf16[16,32,1024]{2,1,0:T(8,128)(2,1)}), bf16[16,32,1024]{2,1,0:T(8,128)(2,1)S(1)}, u32[]{:S(2)}, u32[]{:S(2)}) async-start(bf16[16,32,1024]{2,1,0:T(8,128)(2,1)} %bitcast.9), calls=%async_computation.3 | async-start | bytes 2097152 | tf_op jit(solution)/shard_map/all_to_all | solution.py:473
  191.1 29.9 %collective-permute-start.6 = (bf16[16,32,1024]{2,1,0:T(8,128)(2,1)}, bf16[16,32,1024]{2,1,0:T(8,128)(2,1)}, u32[]{:S(2)}, u32[]{:S(2)}) collective-permute-start(bf16[16,32,1024]{2,1,0:T(8,128)(2,1)} %copy-done.7), channel_id=1, source_target_pairs={{0,16},{16,32},{32,48},{48,0},{1,17},{17,33},{33,49},{49,1},{2,18}... | collective-permute-start | bytes 3145736 | tf_op jit(solution)/shard_map/ppermute | solution.py:477
  194.3 27.1 %collective-permute-start.8 = (bf16[16,32,1024]{2,1,0:T(8,128)(2,1)}, bf16[16,32,1024]{2,1,0:T(8,128)(2,1)}, u32[]{:S(2)}, u32[]{:S(2)}) collective-permute-start(bf16[16,32,1024]{2,1,0:T(8,128)(2,1)} %copy-done.7), channel_id=1, source_target_pairs={{0,48},{16,0},{32,16},{48,32},{1,49},{17,1},{33,17},{49,33},{2,50}... | collective-permute-start | bytes 3145736 | tf_op jit(solution)/shard_map/ppermute | solution.py:477
  208.3 24.1 %copy-start.1 = (bf16[16,32,1024]{2,1,0:T(8,128)(2,1)}, bf16[16,32,1024]{2,1,0:T(8,128)(2,1)S(1)}, u32[]{:S(2)}) copy-start(bf16[16,32,1024]{2,1,0:T(8,128)(2,1)S(1)} %all-to-all-done.3) | copy-start | bytes 3145732
  208.3 35.1 %collective-permute-start.12 = (bf16[16,32,1024]{2,1,0:T(8,128)(2,1)S(1)}, bf16[16,32,1024]{2,1,0:T(8,128)(2,1)S(1)}, u32[]{:S(2)}, u32[]{:S(2)}) collective-permute-start(bf16[16,32,1024]{2,1,0:T(8,128)(2,1)S(1)} %all-to-all-done.3), channel_id=1, source_target_pairs={{0,16},{16,32},{32,48},{48,0},{1,17},{17,33},{33,49},{49,1},{2,18}... | collective-permute-start | bytes 3145736 | tf_op jit(solution)/shard_map/ppermute | solution.py:477
  211.5 31.9 %collective-permute-start.13 = (bf16[16,32,1024]{2,1,0:T(8,128)(2,1)S(1)}, bf16[16,32,1024]{2,1,0:T(8,128)(2,1)}, u32[]{:S(2)}, u32[]{:S(2)}) collective-permute-start(bf16[16,32,1024]{2,1,0:T(8,128)(2,1)S(1)} %all-to-all-done.3), channel_id=1, source_target_pairs={{0,48},{16,0},{32,16},{48,32},{1,49},{17,1},{33,17},{49,33},{2,50}... | collective-permute-start | bytes 3145736 | tf_op jit(solution)/shard_map/ppermute | solution.py:477
  215.2 47.4 %collective-permute-start = (bf16[16,32,1024]{2,1,0:T(8,128)(2,1)S(1)}, bf16[16,32,1024]{2,1,0:T(8,128)(2,1)}, u32[]{:S(2)}, u32[]{:S(2)}) collective-permute-start(bf16[16,32,1024]{2,1,0:T(8,128)(2,1)S(1)} %all-to-all-done.3), channel_id=1, source_target_pairs={{0,64},{64,0},{1,65},{65,1},{2,66},{66,2},{3,67},{67,3},{4,68},{68... | collective-permute-start | bytes 3145736 | tf_op jit(solution)/shard_map/ppermute | solution.py:481
  221.0 44.7 %collective-permute-start.7 = (bf16[16,32,1024]{2,1,0:T(8,128)(2,1)}, bf16[16,32,1024]{2,1,0:T(8,128)(2,1)S(1)}, u32[]{:S(2)}, u32[]{:S(2)}) collective-permute-start(bf16[16,32,1024]{2,1,0:T(8,128)(2,1)} %collective-permute-done.6), channel_id=1, source_target_pairs={{0,64},{64,0},{1,65},{65,1},{2,66},{66,2},{3,67},{67,3},{4,68},{68... | collective-permute-start | bytes 3145736 | tf_op jit(solution)/shard_map/ppermute | solution.py:481
  221.4 62.3 %collective-permute-start.9 = (bf16[16,32,1024]{2,1,0:T(8,128)(2,1)}, bf16[16,32,1024]{2,1,0:T(8,128)(2,1)}, u32[]{:S(2)}, u32[]{:S(2)}) collective-permute-start(bf16[16,32,1024]{2,1,0:T(8,128)(2,1)} %collective-permute-done.8), channel_id=1, source_target_pairs={{0,64},{64,0},{1,65},{65,1},{2,66},{66,2},{3,67},{67,3},{4,68},{68... | collective-permute-start | bytes 3145736 | tf_op jit(solution)/shard_map/ppermute | solution.py:481
  243.4 5.5 %copy-start.3 = (bf16[16,32,1024]{2,1,0:T(8,128)(2,1)}, bf16[16,32,1024]{2,1,0:T(8,128)(2,1)S(1)}, u32[]{:S(2)}) copy-start(bf16[16,32,1024]{2,1,0:T(8,128)(2,1)S(1)} %collective-permute-done.12) | copy-start | bytes 3145732
  243.4 19.6 %collective-permute-start.16 = (bf16[8,32,1024]{2,1,0:T(8,128)(2,1)}, bf16[8,32,1024]{2,1,0:T(8,128)(2,1)}, u32[]{:S(2)}, u32[]{:S(2)}) collective-permute-start(bf16[8,32,1024]{2,1,0:T(8,128)(2,1)} %slice.92), channel_id=1, source_target_pairs={{0,16},{16,32},{32,48},{48,0},{1,17},{17,33},{33,49},{49,1},{2,18}... | collective-permute-start | bytes 1572872 | tf_op jit(solution)/shard_map/ppermute | solution.py:477
  243.4 19.6 %collective-permute-start.17 = (bf16[8,32,1024]{2,1,0:T(8,128)(2,1)}, bf16[8,32,1024]{2,1,0:T(8,128)(2,1)}, u32[]{:S(2)}, u32[]{:S(2)}) collective-permute-start(bf16[8,32,1024]{2,1,0:T(8,128)(2,1)} %slice.93), channel_id=1, source_target_pairs={{0,48},{16,0},{32,16},{48,32},{1,49},{17,1},{33,17},{49,33},{2,50}... | collective-permute-start | bytes 1572872 | tf_op jit(solution)/shard_map/ppermute | solution.py:477
  246.7 10.6 %copy-start.16 = (f32[4,1024]{1,0:T(4,128)S(1)}, f32[4,1024]{1,0:T(4,128)}, u32[]{:S(2)}) copy-start(f32[4,1024]{1,0:T(4,128)} %get-tuple-element.62) | copy-start | bytes 49156
  246.7 10.6 %copy-start.17 = (f32[4,1024]{1,0:T(4,128)S(1)}, f32[4,1024]{1,0:T(4,128)}, u32[]{:S(2)}) copy-start(f32[4,1024]{1,0:T(4,128)} %get-tuple-element.61) | copy-start | bytes 49156
  248.9 116.7 %all-to-all-start.7 = ((bf16[16,128,256]{2,1,0:T(8,128)(2,1)}), bf16[16,128,256]{2,1,0:T(8,128)(2,1)S(1)}, u32[]{:S(2)}, u32[]{:S(2)}) async-start(bf16[16,128,256]{2,1,0:T(8,128)(2,1)} %bitcast.45), calls=%async_computation.7 | async-start | bytes 2097152 | tf_op jit(solution)/shard_map/all_to_all | solution.py:473
  259.6 3.1 copy-start.8
  262.6 66.0 %collective-permute-start.5 = (bf16[16,32,1024]{2,1,0:T(8,128)(2,1)S(1)}, bf16[16,32,1024]{2,1,0:T(8,128)(2,1)S(1)}, u32[]{:S(2)}, u32[]{:S(2)}) collective-permute-start(bf16[16,32,1024]{2,1,0:T(8,128)(2,1)S(1)} %copy-done.8), channel_id=1, source_target_pairs={{0,64},{64,0},{1,65},{65,1},{2,66},{66,2},{3,67},{67,3},{4,68},{68... | collective-permute-start | bytes 3145736 | tf_op jit(solution)/shard_map/ppermute | solution.py:481
  263.0 41.2 %collective-permute-start.14 = (bf16[8,32,1024]{2,1,0:T(8,128)(2,1)S(1)}, bf16[8,32,1024]{2,1,0:T(8,128)(2,1)S(1)}, u32[]{:S(2)}, u32[]{:S(2)}) collective-permute-start(bf16[8,32,1024]{2,1,0:T(8,128)(2,1)S(1)} %slice.90), channel_id=1, source_target_pairs={{0,16},{16,32},{32,48},{48,0},{1,17},{17,33},{33,49},{49,1},{2,18}... | collective-permute-start | bytes 1572872 | tf_op jit(solution)/shard_map/ppermute | solution.py:477
  263.0 41.5 %collective-permute-start.15 = (bf16[8,32,1024]{2,1,0:T(8,128)(2,1)}, bf16[8,32,1024]{2,1,0:T(8,128)(2,1)S(1)}, u32[]{:S(2)}, u32[]{:S(2)}) collective-permute-start(bf16[8,32,1024]{2,1,0:T(8,128)(2,1)} %slice.91), channel_id=1, source_target_pairs={{0,48},{16,0},{32,16},{48,32},{1,49},{17,1},{33,17},{49,33},{2,50}... | collective-permute-start | bytes 1572872 | tf_op jit(solution)/shard_map/ppermute | solution.py:477
  265.7 35.8 %copy-start.2 = (bf16[16,32,1024]{2,1,0:T(8,128)(2,1)}, bf16[16,32,1024]{2,1,0:T(8,128)(2,1)S(1)}, u32[]{:S(2)}) copy-start(bf16[16,32,1024]{2,1,0:T(8,128)(2,1)S(1)} %collective-permute-done.7) | copy-start | bytes 3145732
  265.7 59.2 %collective-permute-start.1 = (bf16[16,32,1024]{2,1,0:T(8,128)(2,1)}, bf16[16,32,1024]{2,1,0:T(8,128)(2,1)S(1)}, u32[]{:S(2)}, u32[]{:S(2)}) collective-permute-start(bf16[16,32,1024]{2,1,0:T(8,128)(2,1)} %collective-permute-done), channel_id=1, source_target_pairs={{0,16},{16,32},{32,48},{48,0},{1,17},{17,33},{33,49},{49,1},{2,18}... | collective-permute-start | bytes 3145736 | tf_op jit(solution)/shard_map/ppermute | solution.py:477
  283.7 41.4 %collective-permute-start.2 = (bf16[16,32,1024]{2,1,0:T(8,128)(2,1)}, bf16[16,32,1024]{2,1,0:T(8,128)(2,1)S(1)}, u32[]{:S(2)}, u32[]{:S(2)}) collective-permute-start(bf16[16,32,1024]{2,1,0:T(8,128)(2,1)} %collective-permute-done), channel_id=1, source_target_pairs={{0,48},{16,0},{32,16},{48,32},{1,49},{17,1},{33,17},{49,33},{2,50}... | collective-permute-start | bytes 3145736 | tf_op jit(solution)/shard_map/ppermute | solution.py:477
  304.2 2.7 copy-start.11
  304.2 24.4 %collective-permute-start.10 = (bf16[8,32,1024]{2,1,0:T(8,128)(2,1)}, bf16[8,32,1024]{2,1,0:T(8,128)(2,1)S(1)}, u32[]{:S(2)}, u32[]{:S(2)}) collective-permute-start(bf16[8,32,1024]{2,1,0:T(8,128)(2,1)} %slice.88), channel_id=1, source_target_pairs={{0,16},{16,32},{32,48},{48,0},{1,17},{17,33},{33,49},{49,1},{2,18}... | collective-permute-start | bytes 1572872 | tf_op jit(solution)/shard_map/ppermute | solution.py:477
  304.5 2.4 copy-start.13
  304.5 24.1 %collective-permute-start.11 = (bf16[8,32,1024]{2,1,0:T(8,128)(2,1)}, bf16[8,32,1024]{2,1,0:T(8,128)(2,1)S(1)}, u32[]{:S(2)}, u32[]{:S(2)}) collective-permute-start(bf16[8,32,1024]{2,1,0:T(8,128)(2,1)} %slice.89), channel_id=1, source_target_pairs={{0,48},{16,0},{32,16},{48,32},{1,49},{17,1},{33,17},{49,33},{2,50}... | collective-permute-start | bytes 1572872 | tf_op jit(solution)/shard_map/ppermute | solution.py:477
  324.9 21.7 %copy-start.4 = (bf16[16,32,1024]{2,1,0:T(8,128)(2,1)}, bf16[16,32,1024]{2,1,0:T(8,128)(2,1)S(1)}, u32[]{:S(2)}) copy-start(bf16[16,32,1024]{2,1,0:T(8,128)(2,1)S(1)} %collective-permute-done.1) | copy-start | bytes 3145732
  325.0 21.6 %collective-permute-start.3 = (bf16[8,32,1024]{2,1,0:T(8,128)(2,1)S(1)}, bf16[8,32,1024]{2,1,0:T(8,128)(2,1)S(1)}, u32[]{:S(2)}, u32[]{:S(2)}) collective-permute-start(bf16[8,32,1024]{2,1,0:T(8,128)(2,1)S(1)} %slice.85), channel_id=1, source_target_pairs={{0,16},{16,32},{32,48},{48,0},{1,17},{17,33},{33,49},{49,1},{2,18}... | collective-permute-start | bytes 1572872 | tf_op jit(solution)/shard_map/ppermute | solution.py:477
  325.1 21.5 %copy-start.5 = (bf16[16,32,1024]{2,1,0:T(8,128)(2,1)}, bf16[16,32,1024]{2,1,0:T(8,128)(2,1)S(1)}, u32[]{:S(2)}) copy-start(bf16[16,32,1024]{2,1,0:T(8,128)(2,1)S(1)} %collective-permute-done.2) | copy-start | bytes 3145732
  326.1 20.5 %collective-permute-start.4 = (bf16[8,32,1024]{2,1,0:T(8,128)(2,1)}, bf16[8,32,1024]{2,1,0:T(8,128)(2,1)S(1)}, u32[]{:S(2)}, u32[]{:S(2)}) collective-permute-start(bf16[8,32,1024]{2,1,0:T(8,128)(2,1)} %slice.86), channel_id=1, source_target_pairs={{0,48},{16,0},{32,16},{48,32},{1,49},{17,1},{33,17},{49,33},{2,50}... | collective-permute-start | bytes 1572872 | tf_op jit(solution)/shard_map/ppermute | solution.py:477
  328.6 1.0 copy-start.6
  328.7 1.2 copy-start.10
  328.7 1.3 copy-start.12
  346.6 0.8 copy-start.14
  346.7 0.9 copy-start.15
  366.5 19.0 %all-to-all-start.8 = ((f32[128,1,16]{2,1,0:T(1,128)}), f32[128,1,16]{2,1,0:T(1,128)S(1)}, u32[]{:S(2)}, u32[]{:S(2)}) async-start(f32[128,1,16]{2,1,0:T(1,128)} %bitcast.46), calls=%async_computation.8 | async-start | bytes 131072 | tf_op jit(solution)/shard_map/all_to_all | solution.py:473
Sparse Core Ops, SparseCore 0:
  40.8 81.2 all-gather.1

commit v3 on v2

--- a/solution.py
+++ b/solution.py
@@ -517,15 +517,19 @@
     down = turned(w_down[0])
 
     args = (here.reshape(1), ssm_in, ssm_grad, b_proj, c_proj, parts, packs, alog, skip)
-    arrived, grads = {}, {}
+    arrived, grads, moved = {}, {}, {}
     for half in (1, 0):
         x_part, bc_part, step_part = span_grads(*args, half)
         grads[half] = (bc_part, step_part)
         if half == 1:
             x_part, gate_rows = lax.optimization_barrier((x_part, gate_rows))
-        moved = a2a(x_part.reshape(16, 256, 256), EXP)
-        rows = expert_rows(moved, weight, first, half)
-        arrived[half] = a2a(rows.reshape(16, 32, 1024), EXP)
+        moved[half] = a2a(x_part.reshape(16, 256, 256), EXP)
+    rows = {}
+    rows[1] = expert_rows(moved[1], weight, first, 1)
+    rows[1], moved[0] = lax.optimization_barrier((rows[1], moved[0]))
+    rows[0] = expert_rows(moved[0], weight, first, 0)
+    for half in (1, 0):
+        arrived[half] = a2a(rows[half].reshape(16, 32, 1024), EXP)
 
     gate_rows = gate_rows.reshape(16, 8, 16).transpose(1, 0, 2)
     gate_rows = gate_rows.astype(F32).reshape(2, 4, 2, 128, 1)
@@ -540,7 +544,7 @@
     local = joined_x(local)
     partner = near_x(partner)
     partner = joined_x(partner)
-    sets = [(1, 0, mine), (0, 0, local), (1, 1, theirs), (0, 1, partner)]
+    sets = [(1, 0, mine), (0, 0, local), (0, 1, partner), (1, 1, theirs)]
 
     x_at, y_at = lax.axis_index("x"), lax.axis_index("yl")
     saved = saved_pre.reshape(2, 4, 2, 128, 2, 896)

time: 396 us -> 417 us (1.053)
  blocking collectives: 28.6 us -> 52.1 us
  waiting for transfers between devices: 111 us -> 123 us
  starting transfers between devices: 81.3 us -> 71.8 us
  local copies, waits for them, and re-layouts: 26.1 us -> 21.5 us
    all_to_all x1 -> x2, blocking collectives: 28.6 us -> 52.1 us  [a2a(): return lax.all_to_all(array, axis, split_axis=0, concat_axis=0, tiled=True)]
    ppermute x14, waiting for transfers between devices: 12.7 us -> 30.8 us  [shifted(): return lax.ppermute(array, 'x', [(i, (i + by) % 4) for i in range(4)])]
    all_to_all x8 -> x7, starting transfers between devices: 54.3 us -> 49.1 us  [a2a(): return lax.all_to_all(array, axis, split_axis=0, concat_axis=0, tiled=True)]
    all_to_all x8 -> x7, waiting for transfers between devices: 80.4 us -> 77.4 us  [a2a(): return lax.all_to_all(array, axis, split_axis=0, concat_axis=0, tiled=True)]
  transfers between devices with their start and end apart: 27 -> 26, of which waited for: 9 -> 10; matrix products, arithmetic and copies ran while one was open for 6% -> 5% of each run, Pallas kernels for 31% -> 28%
where the time goes in v3:
time: 417 us; the launch traced here: 414 us
  Pallas kernels  126 us (30%)
  waiting for transfers between devices  123 us (29%)
  starting transfers between devices  71.8 us (17%)
  blocking collectives  52.1 us (12%)
  local copies, waits for them, and re-layouts  21.5 us (5%)
  between operations  14.4 us (3%)
  other arithmetic  6.03 us (1%)
    all_to_all x7, waiting for transfers between devices, a2a(): return lax.all_to_all(array, axis, split_axis=0, concat_axis=0, tiled=True)  77.4 us
    pallas_call x4, Pallas kernels, expert_grads(): pl.pallas_call(functools.partial(expert_kernel, half), in_specs=[pl.Block...  66.3 us
    all_to_all x2, blocking collectives, a2a(): return lax.all_to_all(array, axis, split_axis=0, concat_axis=0, tiled=True)  52.1 us
    all_to_all x7, starting transfers between devices, a2a(): return lax.all_to_all(array, axis, split_axis=0, concat_axis=0, tiled=True)  49.1 us
    ppermute x14, waiting for transfers between devices, shifted(): return lax.ppermute(array, 'x', [(i, (i + by) % 4) for i in range(4)])  30.8 us
    pallas_call x2, Pallas kernels, span_grads(): pl.pallas_call(grads_kernel, grid=(spans,), in_specs=[pl.BlockSpec(memory...  20.7 us
    ppermute x14, starting transfers between devices, shifted(): return lax.ppermute(array, 'x', [(i, (i + by) % 4) for i in range(4)])  20.5 us
    ppermute x4, waiting for transfers between devices, other_row(): return lax.ppermute(array, 'yl', [(0, 1), (1, 0)])  14.5 us
  transfers between devices with their start and end apart: 26, of which 10 were waited for; matrix products, arithmetic and copies ran while one was open for 5% of the time, Pallas kernels for 28%

profile of v3, /device:TPU:1, one launch (start us, length us, event | category | flops | bytes accessed | tf_op | source)
XLA Modules:
  0.0 414.2 jit_solution(1310704768165959993)
XLA Ops:
  7.2 1.6 routing.1
  8.8 2.6 first_exchange.1
  11.4 28.6 %all_to_all.57.res_ref = bf16[4,176,1024]{2,1,0:T(8,128)(2,1)S(1)} all-to-all(bf16[4,176,1024]{2,1,0:T(8,128)(2,1)} %first_exchange.1), channel_id=1, replica_groups=mesh['yl'=2,'x'=4,'yh'=2,'zh'=2,'zl'=2,'core'=2] {'yh','zh'}, dimensions={0} | all-to-all | bytes 2883584 | tf_op jit(solution)/shard_map/all_to_all | solution.py:473
  41.4 11.1 %states.1 = (f32[16,8,128]{2,1,0:T(8,128)}, f32[16,128,8]{2,1,0:T(8,128)}, bf16[16,256,128]{2,1,0:T(8,128)(2,1)}, bf16[16,256,128]{2,1,0:T(8,128)(2,1)}, f32[16,...) custom-call(bf16[2048,256]{1,0:T(8,128)(2,1)} %x_ref.5, bf16[2048,256]{1,0:T(8,128)(2,1)} %g_ref.5, ...), custom_call_target="tpu_custom_call" | custom-call | flops 8000000000 | bytes 1048576 | tf_op jit(solution)/shard_map/states/pallas_call | solution.py:96
  55.1 4.2 %all-to-all-start.1 = ((bf16[8,288,128]{2,1,0:T(8,128)(2,1)}), bf16[8,288,128]{2,1,0:T(8,128)(2,1)S(1)}, u32[]{:S(2)}, u32[]{:S(2)}) async-start(bf16[8,288,128]{2,1,0:T(8,128)(2,1)} %pad_maximum_fusion.1), calls=%async_computation.1 | async-start | bytes 1179648 | tf_op jit(solution)/shard_map/all_to_all | solution.py:473
  60.0 10.3 %all-to-all-done.1.packs_ref = bf16[8,288,128]{2,1,0:T(8,128)(2,1)S(1)} async-done(((bf16[8,288,128]{2,1,0:T(8,128)(2,1)}), bf16[8,288,128]{2,1,0:T(8,128)(2,1)S(1)}, u32[]{:S(2)}, u32[]{:S(2)}) %all-to-all-start.1) | async-done | bytes 589856 | tf_op jit(solution)/shard_map/all_to_all | solution.py:473
  71.1 7.8 %all-to-all-start.2 = ((bf16[16,1,128]{2,1,0:T(2,128)(2,1)}), bf16[16,1,128]{2,1,0:T(2,128)(2,1)S(1)}, u32[]{:S(2)}, u32[]{:S(2)}) async-start(bf16[16,1,128]{2,1,0:T(2,128)(2,1)} %all_to_all.47), calls=%async_computation.2 | async-start | bytes 16384 | tf_op jit(solution)/shard_map/all_to_all | solution.py:473
  78.9 10.3 %span_grads.2 = (bf16[4,4,2,128,256]{4,3,2,1,0:T(8,128)(2,1)}, bf16[1024,256]{1,0:T(8,128)(2,1)}, f32[4,1024]{1,0:T(4,128)}) custom-call(s32[1]{0:T(128)} %bitcast.2.me_ref, bf16[2048,256]{1,0:T(8,128)(2,1)} %x_ref.5, bf16[2048,256]{1,0:T(8,128)(2,1)} %g_ref.5, bf16[2048,128]{1,0:T(8,128)(2,1)} %b_ref.5, bf16[2048,128]{1,0:T(8,128)(2,1)} %c_ref.5, ...), custom_call_target="tpu_custom_call" | custom-call | flops 5000000000 | bytes 1048576 | tf_op jit(solution)/shard_map/span_grads/pallas_call | solution.py:202
  89.3 7.2 %all-to-all-start.3 = ((bf16[16,256,256]{2,1,0:T(8,128)(2,1)}), bf16[16,256,256]{2,1,0:T(8,128)(2,1)S(1)}, u32[]{:S(2)}, u32[]{:S(2)}) async-start(bf16[16,256,256]{2,1,0:T(8,128)(2,1)} %bitcast.75), calls=%async_computation.3 | async-start | bytes 4194304 | tf_op jit(solution)/shard_map/all_to_all | solution.py:473
  96.5 10.3 %span_grads.3 = (bf16[4,4,2,128,256]{4,3,2,1,0:T(8,128)(2,1)}, bf16[1024,256]{1,0:T(8,128)(2,1)}, f32[4,1024]{1,0:T(4,128)}) custom-call(s32[1]{0:T(128)} %bitcast.2.me_ref, bf16[2048,256]{1,0:T(8,128)(2,1)} %x_ref.5, bf16[2048,256]{1,0:T(8,128)(2,1)} %g_ref.5, bf16[2048,128]{1,0:T(8,128)(2,1)} %b_ref.5, bf16[2048,128]{1,0:T(8,128)(2,1)} %c_ref.5, ...), custom_call_target="tpu_custom_call" | custom-call | flops 5000000000 | bytes 1048576 | tf_op jit(solution)/shard_map/span_grads/pallas_call | solution.py:202
  106.8 20.2 %all-to-all-done.3.x_ref = bf16[16,256,256]{2,1,0:T(8,128)(2,1)S(1)} async-done(((bf16[16,256,256]{2,1,0:T(8,128)(2,1)}), bf16[16,256,256]{2,1,0:T(8,128)(2,1)S(1)}, u32[]{:S(2)}, u32[]{:S(2)}) %all-to-all-start.3) | async-done | bytes 2097184 | tf_op jit(solution)/shard_map/all_to_all | solution.py:473
  127.1 6.2 %all-to-all-start.4 = ((bf16[16,256,256]{2,1,0:T(8,128)(2,1)}), bf16[16,256,256]{2,1,0:T(8,128)(2,1)}, u32[]{:S(2)}, u32[]{:S(2)}) async-start(bf16[16,256,256]{2,1,0:T(8,128)(2,1)} %bitcast.76), calls=%async_computation.4 | async-start | bytes 4194304 | tf_op jit(solution)/shard_map/all_to_all | solution.py:473
  133.3 7.3 %expert_rows.2 = bf16[16,2,16,1024]{3,2,1,0:T(8,128)(2,1)} custom-call(bf16[16,256,256]{2,1,0:T(8,128)(2,1)S(1)} %all-to-all-done.3.x_ref, bf16[8,4,4,32,1024]{4,3,2,1,0:T(8,128)(2,1)} %bitcast.67, bf16[4,176,1024]{2,1,0:T(8,128)(2,1)S(1)} %all_to_all.57.res_ref), custom_call_target="tpu_custom_call" | custom-call | flops 3000000000 | bytes 1048576 | tf_op jit(solution)/shard_map/expert_rows/pallas_call | solution.py:304
  140.6 21.2 %all-to-all-done.4.x_ref = bf16[16,256,256]{2,1,0:T(8,128)(2,1)} async-done(((bf16[16,256,256]{2,1,0:T(8,128)(2,1)}), bf16[16,256,256]{2,1,0:T(8,128)(2,1)}, u32[]{:S(2)}, u32[]{:S(2)}) %all-to-all-start.4) | async-done | bytes 2097184 | tf_op jit(solution)/shard_map/all_to_all | solution.py:473
  161.8 7.1 %expert_rows.3 = bf16[16,2,16,1024]{3,2,1,0:T(8,128)(2,1)S(1)} custom-call(bf16[16,256,256]{2,1,0:T(8,128)(2,1)} %all-to-all-done.4.x_ref, bf16[8,4,4,32,1024]{4,3,2,1,0:T(8,128)(2,1)} %bitcast.68, bf16[4,176,1024]{2,1,0:T(8,128)(2,1)S(1)} %all_to_all.57.res_ref), custom_call_target="tpu_custom_call" | custom-call | flops 3000000000 | bytes 1048576 | tf_op jit(solution)/shard_map/expert_rows/pallas_call | solution.py:304
  168.9 23.5 %all_to_all.58 = bf16[16,32,1024]{2,1,0:T(8,128)(2,1)S(1)} all-to-all(bf16[16,32,1024]{2,1,0:T(8,128)(2,1)S(1)} %bitcast.61), channel_id=1, replica_groups=mesh['yl'=2,'x'=4,'yh'=2,'zh'=2,'zl'=2,'core'=2] {'yh','zh','zl','core'}, dimensions={0} | all-to-all | bytes 2097152 | tf_op jit(solution)/shard_map/all_to_all | solution.py:473
  192.4 5.3 %all-to-all-start.5 = ((bf16[16,32,1024]{2,1,0:T(8,128)(2,1)}), bf16[16,32,1024]{2,1,0:T(8,128)(2,1)}, u32[]{:S(2)}, u32[]{:S(2)}) async-start(bf16[16,32,1024]{2,1,0:T(8,128)(2,1)} %bitcast.11), calls=%async_computation.5 | async-start | bytes 2097152 | tf_op jit(solution)/shard_map/all_to_all | solution.py:473
  198.3 16.7 %all-to-all-done.5 = bf16[16,32,1024]{2,1,0:T(8,128)(2,1)} async-done(((bf16[16,32,1024]{2,1,0:T(8,128)(2,1)}), bf16[16,32,1024]{2,1,0:T(8,128)(2,1)}, u32[]{:S(2)}, u32[]{:S(2)}) %all-to-all-start.5) | async-done | bytes 1048608 | tf_op jit(solution)/shard_map/all_to_all | solution.py:473
  215.0 3.1 collective-permute-start.1
  218.1 3.4 collective-permute-start.3
  222.2 2.7 collective-permute-start.13
  224.8 8.4 %collective-permute-done.7 = bf16[16,32,1024]{2,1,0:T(8,128)(2,1)} collective-permute-done((bf16[16,32,1024]{2,1,0:T(8,128)(2,1)S(1)}, bf16[16,32,1024]{2,1,0:T(8,128)(2,1)}, u32[]{:S(2)}, u32[]{:S(2)}) %collective-permute-start.7) | collective-permute-done | bytes 1048608 | tf_op jit(solution)/shard_map/ppermute | solution.py:481
  233.3 2.7 collective-permute-start.8
  236.7 9.1 %turned.1.w_hbm = bf16[896,4096]{1,0:T(8,128)(2,1)} custom-call(bf16[896,4096]{1,0:T(8,128)(2,1)} %bitcast.69), custom_call_target="tpu_custom_call" | custom-call | flops 3000000000 | bytes 1048576 | tf_op jit(solution)/shard_map/turned/pallas_call | solution.py:332
  245.8 1.9 slice.92
  247.7 1.9 slice.93
  249.6 3.0 collective-permute-start.17
  252.5 13.6 %collective-permute-done.12 = bf16[16,32,1024]{2,1,0:T(8,128)(2,1)S(1)} collective-permute-done((bf16[16,32,1024]{2,1,0:T(8,128)(2,1)S(1)}, bf16[16,32,1024]{2,1,0:T(8,128)(2,1)S(1)}, u32[]{:S(2)}, u32[]{:S(2)}) %collective-permute-start.12) | collective-permute-done | bytes 1048608 | tf_op jit(solution)/shard_map/ppermute | solution.py:477
  266.2 1.3 collective-permute-start.9
  268.1 2.2 pad_maximum_fusion
  270.4 8.0 %all-to-all-start.7 = ((bf16[16,128,256]{2,1,0:T(8,128)(2,1)}), bf16[16,128,256]{2,1,0:T(8,128)(2,1)S(1)}, u32[]{:S(2)}, u32[]{:S(2)}) async-start(bf16[16,128,256]{2,1,0:T(8,128)(2,1)} %bitcast.45), calls=%async_computation.7 | async-start | bytes 2097152 | tf_op jit(solution)/shard_map/all_to_all | solution.py:473
  279.1 1.5 reshape.170.gates
  280.6 1.1 slice.90
  281.8 1.1 slice.91
  282.9 17.1 %collective-permute-done.16 = bf16[8,32,1024]{2,1,0:T(8,128)(2,1)} collective-permute-done((bf16[8,32,1024]{2,1,0:T(8,128)(2,1)}, bf16[8,32,1024]{2,1,0:T(8,128)(2,1)}, u32[]{:S(2)}, u32[]{:S(2)}) %collective-permute-start.16) | collective-permute-done | bytes 524320 | tf_op jit(solution)/shard_map/ppermute | solution.py:477
  300.0 1.2 collective-permute-start.15
  301.2 1.5 collective-permute-start.4
  302.6 16.6 %expert_grads.4 = (bf16[2,4,2,128,2,896]{5,4,3,2,1,0:T(2,128)(2,1)}, f32[8,512]{1,0:T(8,128)}) custom-call(s32[2]{0:T(128)} %pad_add_fusion.1.at_ref, bf16[4,4,2,16,1024]{4,3,2,1,0:T(8,128)(2,1)} %bitcast.32.own, bf16[4,4,2,16,1024]{4,3,2,1,0:T(8,128)(2,1)} %bitcast.33.left, bf16[4,4,2,16,1024]{4,3,2,1,0:T(8,128)(2,1)} %bitcast.34.right, ...), custom_call_target="tpu_custom_call" | custom-call | flops 6000000000 | bytes 1048576 | tf_op jit(solution)/shard_map/expert_grads/pallas_call | solution.py:437
  319.5 1.1 slice.89
  321.0 2.4 collective-permute-start.11
  323.4 16.6 %expert_grads.5 = (bf16[2,4,2,128,2,896]{5,4,3,2,1,0:T(2,128)(2,1)}, f32[8,512]{1,0:T(8,128)}) custom-call(s32[2]{0:T(128)} %pad_add_fusion.1.at_ref, bf16[4,4,2,16,1024]{4,3,2,1,0:T(8,128)(2,1)} %bitcast.70, bf16[4,4,2,16,1024]{4,3,2,1,0:T(8,128)(2,1)} %bitcast.72, bf16[4,4,2,16,1024]{4,3,2,1,0:T(8,128)(2,1)} %bitcast.29.right, ...), custom_call_target="tpu_custom_call", output_to_operand_aliasing={{0}: (9, {})} | custom-call | flops 6000000000 | bytes 1048576 | tf_op jit(solution)/shard_map/expert_grads/pallas_call | solution.py:437
  341.5 2.4 collective-permute-done.4
  346.1 16.6 %expert_grads.6 = (bf16[2,4,2,128,2,896]{5,4,3,2,1,0:T(2,128)(2,1)}, f32[8,512]{1,0:T(8,128)}) custom-call(s32[2]{0:T(128)} %pad_add_fusion.at_ref, bf16[4,4,2,16,1024]{4,3,2,1,0:T(8,128)(2,1)} %bitcast.21.own, bf16[4,4,2,16,1024]{4,3,2,1,0:T(8,128)(2,1)} %bitcast.71, bf16[4,4,2,16,1024]{4,3,2,1,0:T(8,128)(2,1)} %bitcast.23.right, ...), custom_call_target="tpu_custom_call", output_to_operand_aliasing={{0}: (9, {})} | custom-call | flops 6000000000 | bytes 1048576 | tf_op jit(solution)/shard_map/expert_grads/pallas_call | solution.py:437
  362.7 3.7 collective-permute-done
  366.4 1.0 copy-done.5
  367.7 16.6 %expert_grads.7 = (bf16[2,4,2,128,2,896]{5,4,3,2,1,0:T(2,128)(2,1)}, f32[8,512]{1,0:T(8,128)}) custom-call(s32[2]{0:T(128)} %pad_add_fusion.at_ref, bf16[4,4,2,16,1024]{4,3,2,1,0:T(8,128)(2,1)} %bitcast.77, bf16[4,4,2,16,1024]{4,3,2,1,0:T(8,128)(2,1)} %bitcast.73, bf16[4,4,2,16,1024]{4,3,2,1,0:T(8,128)(2,1)} %bitcast.74, ...), custom_call_target="tpu_custom_call", output_to_operand_aliasing={{0}: (9, {})} | custom-call | flops 6000000000 | bytes 1048576 | tf_op jit(solution)/shard_map/expert_grads/pallas_call | solution.py:437
  386.6 10.4 %all-to-all-start.8 = ((f32[128,1,16]{2,1,0:T(1,128)}), f32[128,1,16]{2,1,0:T(1,128)S(1)}, u32[]{:S(2)}, u32[]{:S(2)}) async-start(f32[128,1,16]{2,1,0:T(1,128)} %bitcast.46), calls=%async_computation.8 | async-start | bytes 131072 | tf_op jit(solution)/shard_map/all_to_all | solution.py:473
  397.6 9.0 %all-to-all-done.8 = f32[128,1,16]{2,1,0:T(1,128)S(1)} async-done(((f32[128,1,16]{2,1,0:T(1,128)}), f32[128,1,16]{2,1,0:T(1,128)S(1)}, u32[]{:S(2)}, u32[]{:S(2)}) %all-to-all-start.8) | async-done | bytes 8224 | tf_op jit(solution)/shard_map/all_to_all | solution.py:473
  (99 shorter events, 17.4 us)
Async XLA Ops:
  7.2 126.2 %all-gather.2.cloned.1.call-start = ((), (), s32[]{:S(2)}) async-start(), calls=%async_computation.9 | async-start | bytes 8650752 | tf_op jit(solution)/shard_map/all_gather | solution.py:502
  11.4 29.4 %copy-start.16 = (f32[4]{0:T(128)S(1)}, f32[4]{0:T(128)}, u32[]{:S(2)}) copy-start(f32[4]{0:T(128)} %param.23) | copy-start | bytes 52
  41.4 11.8 %copy-start.15 = (bf16[16,16]{1,0:T(8,128)(2,1)S(1)}, bf16[16,16]{1,0:T(8,128)(2,1)}, u32[]{:S(2)}) copy-start(bf16[16,16]{1,0:T(8,128)(2,1)} %get-tuple-element.45) | copy-start | bytes 1540
  52.5 6.7 %copy-start.17 = (f32[4]{0:T(128)S(1)}, f32[4]{0:T(128)}, u32[]{:S(2)}) copy-start(f32[4]{0:T(128)} %param.24) | copy-start | bytes 52
  55.1 15.2 %all-to-all-start.1 = ((bf16[8,288,128]{2,1,0:T(8,128)(2,1)}), bf16[8,288,128]{2,1,0:T(8,128)(2,1)S(1)}, u32[]{:S(2)}, u32[]{:S(2)}) async-start(bf16[8,288,128]{2,1,0:T(8,128)(2,1)} %pad_maximum_fusion.1), calls=%async_computation.1 | async-start | bytes 1179648 | tf_op jit(solution)/shard_map/all_to_all | solution.py:473
  70.3 8.7 %copy-start.6 = (bf16[8,288,128]{2,1,0:T(8,128)(2,1)}, bf16[8,288,128]{2,1,0:T(8,128)(2,1)S(1)}, u32[]{:S(2)}) copy-start(bf16[8,288,128]{2,1,0:T(8,128)(2,1)S(1)} %all-to-all-done.1.packs_ref) | copy-start | bytes 1769476
  71.1 18.2 %all-to-all-start.2 = ((bf16[16,1,128]{2,1,0:T(2,128)(2,1)}), bf16[16,1,128]{2,1,0:T(2,128)(2,1)S(1)}, u32[]{:S(2)}, u32[]{:S(2)}) async-start(bf16[16,1,128]{2,1,0:T(2,128)(2,1)} %all_to_all.47), calls=%async_computation.2 | async-start | bytes 16384 | tf_op jit(solution)/shard_map/all_to_all | solution.py:473
  89.3 37.8 %all-to-all-start.3 = ((bf16[16,256,256]{2,1,0:T(8,128)(2,1)}), bf16[16,256,256]{2,1,0:T(8,128)(2,1)S(1)}, u32[]{:S(2)}, u32[]{:S(2)}) async-start(bf16[16,256,256]{2,1,0:T(8,128)(2,1)} %bitcast.75), calls=%async_computation.3 | async-start | bytes 4194304 | tf_op jit(solution)/shard_map/all_to_all | solution.py:473
  127.1 34.7 %all-to-all-start.4 = ((bf16[16,256,256]{2,1,0:T(8,128)(2,1)}), bf16[16,256,256]{2,1,0:T(8,128)(2,1)}, u32[]{:S(2)}, u32[]{:S(2)}) async-start(bf16[16,256,256]{2,1,0:T(8,128)(2,1)} %bitcast.76), calls=%async_computation.4 | async-start | bytes 4194304 | tf_op jit(solution)/shard_map/all_to_all | solution.py:473
  192.4 53.4 %copy-start = (bf16[16,32,1024]{2,1,0:T(8,128)(2,1)}, bf16[16,32,1024]{2,1,0:T(8,128)(2,1)S(1)}, u32[]{:S(2)}) copy-start(bf16[16,32,1024]{2,1,0:T(8,128)(2,1)S(1)} %all_to_all.58) | copy-start | bytes 3145732
  192.4 22.6 %all-to-all-start.5 = ((bf16[16,32,1024]{2,1,0:T(8,128)(2,1)}), bf16[16,32,1024]{2,1,0:T(8,128)(2,1)}, u32[]{:S(2)}, u32[]{:S(2)}) async-start(bf16[16,32,1024]{2,1,0:T(8,128)(2,1)} %bitcast.11), calls=%async_computation.5 | async-start | bytes 2097152 | tf_op jit(solution)/shard_map/all_to_all | solution.py:473
  197.7 35.5 %collective-permute-start.7 = (bf16[16,32,1024]{2,1,0:T(8,128)(2,1)S(1)}, bf16[16,32,1024]{2,1,0:T(8,128)(2,1)}, u32[]{:S(2)}, u32[]{:S(2)}) collective-permute-start(bf16[16,32,1024]{2,1,0:T(8,128)(2,1)S(1)} %all_to_all.58), channel_id=1, source_target_pairs={{0,64},{64,0},{1,65},{65,1},{2,66},{66,2},{3,67},{67,3},{4,68},{68... | collective-permute-start | bytes 3145736 | tf_op jit(solution)/shard_map/ppermute | solution.py:481
  215.0 30.8 %collective-permute-start.1 = (bf16[16,32,1024]{2,1,0:T(8,128)(2,1)}, bf16[16,32,1024]{2,1,0:T(8,128)(2,1)}, u32[]{:S(2)}, u32[]{:S(2)}) collective-permute-start(bf16[16,32,1024]{2,1,0:T(8,128)(2,1)} %all-to-all-done.5), channel_id=1, source_target_pairs={{0,16},{16,32},{32,48},{48,0},{1,17},{17,33},{33,49},{49,1},{2,18}... | collective-permute-start | bytes 3145736 | tf_op jit(solution)/shard_map/ppermute | solution.py:477
  218.1 29.6 %collective-permute-start.3 = (bf16[16,32,1024]{2,1,0:T(8,128)(2,1)}, bf16[16,32,1024]{2,1,0:T(8,128)(2,1)}, u32[]{:S(2)}, u32[]{:S(2)}) collective-permute-start(bf16[16,32,1024]{2,1,0:T(8,128)(2,1)} %all-to-all-done.5), channel_id=1, source_target_pairs={{0,48},{16,0},{32,16},{48,32},{1,49},{17,1},{33,17},{49,33},{2,50}... | collective-permute-start | bytes 3145736 | tf_op jit(solution)/shard_map/ppermute | solution.py:477
  221.5 44.7 %collective-permute-start.12 = (bf16[16,32,1024]{2,1,0:T(8,128)(2,1)S(1)}, bf16[16,32,1024]{2,1,0:T(8,128)(2,1)S(1)}, u32[]{:S(2)}, u32[]{:S(2)}) collective-permute-start(bf16[16,32,1024]{2,1,0:T(8,128)(2,1)S(1)} %all_to_all.58), channel_id=1, source_target_pairs={{0,16},{16,32},{32,48},{48,0},{1,17},{17,33},{33,49},{49,1},{2,18}... | collective-permute-start | bytes 3145736 | tf_op jit(solution)/shard_map/ppermute | solution.py:477
  222.2 59.6 %collective-permute-start.13 = (bf16[16,32,1024]{2,1,0:T(8,128)(2,1)S(1)}, bf16[16,32,1024]{2,1,0:T(8,128)(2,1)}, u32[]{:S(2)}, u32[]{:S(2)}) collective-permute-start(bf16[16,32,1024]{2,1,0:T(8,128)(2,1)S(1)} %all_to_all.58), channel_id=1, source_target_pairs={{0,48},{16,0},{32,16},{48,32},{1,49},{17,1},{33,17},{49,33},{2,50}... | collective-permute-start | bytes 3145736 | tf_op jit(solution)/shard_map/ppermute | solution.py:477
  233.3 67.9 %collective-permute-start.8 = (bf16[16,32,1024]{2,1,0:T(8,128)(2,1)}, bf16[16,32,1024]{2,1,0:T(8,128)(2,1)S(1)}, u32[]{:S(2)}, u32[]{:S(2)}) collective-permute-start(bf16[16,32,1024]{2,1,0:T(8,128)(2,1)} %collective-permute-done.7), channel_id=1, source_target_pairs={{0,16},{16,32},{32,48},{48,0},{1,17},{17,33},{33,49},{49,1},{2,18}... | collective-permute-start | bytes 3145736 | tf_op jit(solution)/shard_map/ppermute | solution.py:477
  247.7 52.3 %collective-permute-start.16 = (bf16[8,32,1024]{2,1,0:T(8,128)(2,1)}, bf16[8,32,1024]{2,1,0:T(8,128)(2,1)}, u32[]{:S(2)}, u32[]{:S(2)}) collective-permute-start(bf16[8,32,1024]{2,1,0:T(8,128)(2,1)} %slice.92), channel_id=1, source_target_pairs={{0,16},{16,32},{32,48},{48,0},{1,17},{17,33},{33,49},{49,1},{2,18}... | collective-permute-start | bytes 1572872 | tf_op jit(solution)/shard_map/ppermute | solution.py:477
  249.6 51.6 %collective-permute-start.17 = (bf16[8,32,1024]{2,1,0:T(8,128)(2,1)}, bf16[8,32,1024]{2,1,0:T(8,128)(2,1)}, u32[]{:S(2)}, u32[]{:S(2)}) collective-permute-start(bf16[8,32,1024]{2,1,0:T(8,128)(2,1)} %slice.93), channel_id=1, source_target_pairs={{0,48},{16,0},{32,16},{48,32},{1,49},{17,1},{33,17},{49,33},{2,50}... | collective-permute-start | bytes 1572872 | tf_op jit(solution)/shard_map/ppermute | solution.py:477
  266.2 4.2 %copy-start.2 = (bf16[16,32,1024]{2,1,0:T(8,128)(2,1)}, bf16[16,32,1024]{2,1,0:T(8,128)(2,1)S(1)}, u32[]{:S(2)}) copy-start(bf16[16,32,1024]{2,1,0:T(8,128)(2,1)S(1)} %collective-permute-done.12) | copy-start | bytes 3145732
  266.2 53.1 %collective-permute-start.9 = (bf16[16,32,1024]{2,1,0:T(8,128)(2,1)}, bf16[16,32,1024]{2,1,0:T(8,128)(2,1)}, u32[]{:S(2)}, u32[]{:S(2)}) collective-permute-start(bf16[16,32,1024]{2,1,0:T(8,128)(2,1)} %collective-permute-done.7), channel_id=1, source_target_pairs={{0,48},{16,0},{32,16},{48,32},{1,49},{17,1},{33,17},{49,33},{2,50}... | collective-permute-start | bytes 3145736 | tf_op jit(solution)/shard_map/ppermute | solution.py:477
  268.1 10.2 %copy-start.13 = (f32[4,1024]{1,0:T(4,128)S(1)}, f32[4,1024]{1,0:T(4,128)}, u32[]{:S(2)}) copy-start(f32[4,1024]{1,0:T(4,128)} %get-tuple-element.66) | copy-start | bytes 49156
  268.1 10.3 %copy-start.14 = (f32[4,1024]{1,0:T(4,128)S(1)}, f32[4,1024]{1,0:T(4,128)}, u32[]{:S(2)}) copy-start(f32[4,1024]{1,0:T(4,128)} %get-tuple-element.65) | copy-start | bytes 49156
  270.4 115.4 %all-to-all-start.7 = ((bf16[16,128,256]{2,1,0:T(8,128)(2,1)}), bf16[16,128,256]{2,1,0:T(8,128)(2,1)S(1)}, u32[]{:S(2)}, u32[]{:S(2)}) async-start(bf16[16,128,256]{2,1,0:T(8,128)(2,1)} %bitcast.45), calls=%async_computation.7 | async-start | bytes 2097152 | tf_op jit(solution)/shard_map/all_to_all | solution.py:473
  281.7 38.9 %collective-permute-start.14 = (bf16[8,32,1024]{2,1,0:T(8,128)(2,1)S(1)}, bf16[8,32,1024]{2,1,0:T(8,128)(2,1)S(1)}, u32[]{:S(2)}, u32[]{:S(2)}) collective-permute-start(bf16[8,32,1024]{2,1,0:T(8,128)(2,1)S(1)} %slice.90), channel_id=1, source_target_pairs={{0,16},{16,32},{32,48},{48,0},{1,17},{17,33},{33,49},{49,1},{2,18}... | collective-permute-start | bytes 1572872 | tf_op jit(solution)/shard_map/ppermute | solution.py:477
  300.0 21.0 %collective-permute-start.15 = (bf16[8,32,1024]{2,1,0:T(8,128)(2,1)S(1)}, bf16[8,32,1024]{2,1,0:T(8,128)(2,1)S(1)}, u32[]{:S(2)}, u32[]{:S(2)}) collective-permute-start(bf16[8,32,1024]{2,1,0:T(8,128)(2,1)S(1)} %slice.91), channel_id=1, source_target_pairs={{0,48},{16,0},{32,16},{48,32},{1,49},{17,1},{33,17},{49,33},{2,50}... | collective-permute-start | bytes 1572872 | tf_op jit(solution)/shard_map/ppermute | solution.py:477
  301.2 40.2 %collective-permute-start.2 = (bf16[16,32,1024]{2,1,0:T(8,128)(2,1)}, bf16[16,32,1024]{2,1,0:T(8,128)(2,1)S(1)}, u32[]{:S(2)}, u32[]{:S(2)}) collective-permute-start(bf16[16,32,1024]{2,1,0:T(8,128)(2,1)} %collective-permute-done.1), channel_id=1, source_target_pairs={{0,64},{64,0},{1,65},{65,1},{2,66},{66,2},{3,67},{67,3},{4,68},{68... | collective-permute-start | bytes 3145736 | tf_op jit(solution)/shard_map/ppermute | solution.py:481
  301.2 18.0 %copy-start.1 = (bf16[16,32,1024]{2,1,0:T(8,128)(2,1)}, bf16[16,32,1024]{2,1,0:T(8,128)(2,1)S(1)}, u32[]{:S(2)}) copy-start(bf16[16,32,1024]{2,1,0:T(8,128)(2,1)S(1)} %collective-permute-done.8) | copy-start | bytes 3145732
  301.2 42.7 %collective-permute-start.4 = (bf16[16,32,1024]{2,1,0:T(8,128)(2,1)}, bf16[16,32,1024]{2,1,0:T(8,128)(2,1)S(1)}, u32[]{:S(2)}, u32[]{:S(2)}) collective-permute-start(bf16[16,32,1024]{2,1,0:T(8,128)(2,1)} %collective-permute-done.3), channel_id=1, source_target_pairs={{0,64},{64,0},{1,65},{65,1},{2,66},{66,2},{3,67},{67,3},{4,68},{68... | collective-permute-start | bytes 3145736 | tf_op jit(solution)/shard_map/ppermute | solution.py:481
  319.3 47.1 %collective-permute-start = (bf16[16,32,1024]{2,1,0:T(8,128)(2,1)}, bf16[16,32,1024]{2,1,0:T(8,128)(2,1)S(1)}, u32[]{:S(2)}, u32[]{:S(2)}) collective-permute-start(bf16[16,32,1024]{2,1,0:T(8,128)(2,1)} %all-to-all-done.5), channel_id=1, source_target_pairs={{0,64},{64,0},{1,65},{65,1},{2,66},{66,2},{3,67},{67,3},{4,68},{68... | collective-permute-start | bytes 3145736 | tf_op jit(solution)/shard_map/ppermute | solution.py:481
  320.6 2.8 copy-start.7
  320.6 24.5 %collective-permute-start.10 = (bf16[8,32,1024]{2,1,0:T(8,128)(2,1)S(1)}, bf16[8,32,1024]{2,1,0:T(8,128)(2,1)S(1)}, u32[]{:S(2)}, u32[]{:S(2)}) collective-permute-start(bf16[8,32,1024]{2,1,0:T(8,128)(2,1)S(1)} %slice.88), channel_id=1, source_target_pairs={{0,16},{16,32},{32,48},{48,0},{1,17},{17,33},{33,49},{49,1},{2,18}... | collective-permute-start | bytes 1572872 | tf_op jit(solution)/shard_map/ppermute | solution.py:477
  321.0 2.4 copy-start.9
  321.0 24.2 %collective-permute-start.11 = (bf16[8,32,1024]{2,1,0:T(8,128)(2,1)S(1)}, bf16[8,32,1024]{2,1,0:T(8,128)(2,1)S(1)}, u32[]{:S(2)}, u32[]{:S(2)}) collective-permute-start(bf16[8,32,1024]{2,1,0:T(8,128)(2,1)S(1)} %slice.89), channel_id=1, source_target_pairs={{0,48},{16,0},{32,16},{48,32},{1,49},{17,1},{33,17},{49,33},{2,50}... | collective-permute-start | bytes 1572872 | tf_op jit(solution)/shard_map/ppermute | solution.py:477
  341.4 21.3 %copy-start.3 = (bf16[16,32,1024]{2,1,0:T(8,128)(2,1)}, bf16[16,32,1024]{2,1,0:T(8,128)(2,1)S(1)}, u32[]{:S(2)}) copy-start(bf16[16,32,1024]{2,1,0:T(8,128)(2,1)S(1)} %collective-permute-done.2) | copy-start | bytes 3145732
  341.4 25.0 %collective-permute-start.5 = (bf16[8,32,1024]{2,1,0:T(8,128)(2,1)S(1)}, bf16[8,32,1024]{2,1,0:T(8,128)(2,1)S(1)}, u32[]{:S(2)}, u32[]{:S(2)}) collective-permute-start(bf16[8,32,1024]{2,1,0:T(8,128)(2,1)S(1)} %slice.86), channel_id=1, source_target_pairs={{0,16},{16,32},{32,48},{48,0},{1,17},{17,33},{33,49},{49,1},{2,18}... | collective-permute-start | bytes 1572872 | tf_op jit(solution)/shard_map/ppermute | solution.py:477
  343.9 18.8 %copy-start.4 = (bf16[16,32,1024]{2,1,0:T(8,128)(2,1)}, bf16[16,32,1024]{2,1,0:T(8,128)(2,1)S(1)}, u32[]{:S(2)}) copy-start(bf16[16,32,1024]{2,1,0:T(8,128)(2,1)S(1)} %collective-permute-done.4) | copy-start | bytes 3145732
  344.8 21.6 %collective-permute-start.6 = (bf16[8,32,1024]{2,1,0:T(8,128)(2,1)}, bf16[8,32,1024]{2,1,0:T(8,128)(2,1)S(1)}, u32[]{:S(2)}, u32[]{:S(2)}) collective-permute-start(bf16[8,32,1024]{2,1,0:T(8,128)(2,1)} %slice.87), channel_id=1, source_target_pairs={{0,48},{16,0},{32,16},{48,32},{1,49},{17,1},{33,17},{49,33},{2,50}... | collective-permute-start | bytes 1572872 | tf_op jit(solution)/shard_map/ppermute | solution.py:477
  345.1 0.8 copy-start.8
  345.1 1.0 copy-start.10
  366.4 1.0 copy-start.5
  366.4 1.2 copy-start.11
  366.4 1.3 copy-start.12
  386.6 20.0 %all-to-all-start.8 = ((f32[128,1,16]{2,1,0:T(1,128)}), f32[128,1,16]{2,1,0:T(1,128)S(1)}, u32[]{:S(2)}, u32[]{:S(2)}) async-start(f32[128,1,16]{2,1,0:T(1,128)} %bitcast.46), calls=%async_computation.8 | async-start | bytes 131072 | tf_op jit(solution)/shard_map/all_to_all | solution.py:473
Sparse Core Ops, SparseCore 0:
  40.8 82.0 all-gather.1
